TPU v7x, 32 devices: a whole 2x2x4 slice. The times are simulated.
32 devices in a mesh: blk: 16 (over z, y, x), obs: 2 (over core).
Axes of the slice: x: 2, y: 2, z: 4, core: 2. Of those that a mesh axis runs over, the one named last changes fastest.
Arguments:
- populations: float32 [16, 19, 32, 1024], P('blk', None, 'obs'), may hold values from 0.011111111 to 0.533333333, as said below
- block_faces: int32 [16, 4], P('blk'), may hold values from 0 to 15, as said below
- block_edges: int32 [16, 4], P('blk'), may hold values from 0 to 15, as said below
- probe_cell: int32 [4096], P(('blk', 'obs')), may hold values from 0 to 16383
- history: bfloat16 [4096, 512], P(('blk', 'obs')), may hold values from -6 to 6
- panel_count: int32 [32], P(('blk', 'obs')), may hold values from 0 to 128, as said below
- panel_owner: int32 [4096], P(('blk', 'obs')), may hold values from 0 to 1023, as said below
- panel_pos: bfloat16 [3, 2048], P(None, ('blk', 'obs')), may hold values from -1 to 1
- panel_normal: bfloat16 [3, 2048], P(None, ('blk', 'obs')), may hold values from -0.625 to 0.625
- observers: float32 [3, 1024], P(None, 'obs'), may hold values from -8 to 8, as said below
Outputs:
- populations_out: float32 [16, 19, 32, 1024], P('blk', None, 'obs')
- spectrum: float32 [2, 512, 128], P('obs', 'blk')
Inputs may be any that keep to these rules, and one draw needn't show every extreme that they name: `populations`: every population is positive. The blocks form a lattice of 4 by 4 blocks along y and z, periodic in both, one block deep in x; block_faces[b] names the blocks beside b at -y, +y, -z, +z. block_edges[b] names the blocks at (-y,-z), (-y,+z), (+y,-z), (+y,+z) of b: the y neighbour's z neighbour, which is the z neighbour's y neighbour. The eight face and edge neighbours of a block are distinct and differ from it. The live slots of a device are its first panel_count slots. The counts of the devices at one obs index sum to 1024. `panel_owner`: in a live slot of the device at blk index b and obs index o the value is q * 64 + j: slot j of the owner at blk index q and the same obs index. Every owner slot receives exactly one live panel. A device sends at most 8 live panels to one owner, and its live panels go to the owners in numbers that differ by at most one. Dead slots hold arbitrary values of the range. `observers`: every observer lies at a distance of 4 to 8 from the anchor (0, 0, 0).
All inputs are finite; a program needn't handle non-finite values.
Results may differ from a plain program's by a relative error of at most 0.0032.
The roundings to bfloat16 on the way count: a program that leaves them out, or rounds other values in their place, can miss the bound.
Values may be sent and summed in bfloat16 or wider, within the bound.
A program may use at most 128 MiB of HBM per device.

v0:
```python
import functools
import math

import jax
import jax.numpy as jnp
from jax import lax
from jax.experimental import pallas as pl
from jax.experimental.pallas import tpu as pltpu
from jax.sharding import PartitionSpec as P

BS = 32
STEPS = 4
SAMPLES = 256
BINS = 64
P_OWN = 64


velocity_list = [
    (0, 0, 0),
    (1, 0, 0),
    (-1, 0, 0),
    (0, 1, 0),
    (0, -1, 0),
    (0, 0, 1),
    (0, 0, -1),
    (1, 1, 0),
    (-1, -1, 0),
    (1, -1, 0),
    (-1, 1, 0),
    (1, 0, 1),
    (-1, 0, -1),
    (1, 0, -1),
    (-1, 0, 1),
    (0, 1, 1),
    (0, -1, -1),
    (0, 1, -1),
    (0, -1, 1),
]
weight_list = [1.0 / 3.0] + [1.0 / 18.0] * 6 + [1.0 / 36.0] * 12
x_moving = [1, 2, 7, 8, 9, 10, 11, 12, 13, 14]
y_upward = [3, 7, 10, 15, 17]
y_downward = [4, 8, 9, 16, 18]
z_upward = [5, 11, 14, 15, 18]
z_downward = [6, 12, 13, 16, 17]
relax_rate = 1.6
pressure_gain = 60.0
sound_speed = 0.5


x_plus = [1, 7, 9, 11, 13]
x_minus = [2, 8, 10, 12, 14]
x_order = x_plus + x_minus
still = [0, 3, 4, 5, 6, 15, 16, 17, 18]
LANES = 128
FACE = 256


def collide_tile(f):
    density = f[0]
    for part in f[1:]:
        density = density + part
    speeds = []
    for axis in range(3):
        plus = None
        minus = None
        for number, velocity in enumerate(velocity_list):
            if velocity[axis] == 1:
                plus = f[number] if plus is None else plus + f[number]
            elif velocity[axis] == -1:
                minus = f[number] if minus is None else minus + f[number]
        speeds.append(plus - minus)
    inverse = 1.0 / density
    speeds = [speed * inverse for speed in speeds]
    squared = speeds[0] * speeds[0] + speeds[1] * speeds[1] + speeds[2] * speeds[2]
    base = 1.0 - 1.5 * squared
    scaled = {}
    for weight in sorted(set(weight_list)):
        scaled[weight] = (relax_rate * weight) * density
    out = []
    for number, velocity in enumerate(velocity_list):
        projected = None
        for axis in range(3):
            if velocity[axis] == 0:
                continue
            if projected is None:
                projected = speeds[axis] if velocity[axis] == 1 else -speeds[axis]
            elif velocity[axis] == 1:
                projected = projected + speeds[axis]
            else:
                projected = projected - speeds[axis]
        bracket = base
        if projected is not None:
            bracket = base + projected * (3.0 + 4.5 * projected)
        out.append((1.0 - relax_rate) * f[number] + scaled[weight_list[number]] * bracket)
    return out, density


def collide_all(field_ref, still_ref, moving_ref, up_ref, down_ref):
    depth = still_ref.shape[1]

    def one_tile(tile, carry):
        lanes = pl.ds(pl.multiple_of(tile * LANES, LANES), LANES)
        out = collide_tile([field_ref[number, :, lanes] for number in range(19)])[0]
        for place, number in enumerate(still):
            still_ref[place, :, lanes] = out[number]
        for place, number in enumerate(x_order):
            moving_ref[place, :, lanes] = out[number]
        for place, number in enumerate(x_plus):
            up_ref[place, :, lanes] = out[number][depth - 1 : depth]
        for place, number in enumerate(x_minus):
            down_ref[place, :, lanes] = out[number][0:1]
        return carry

    lax.fori_loop(0, still_ref.shape[2] // LANES, one_tile, 0)


def lane_of(shape):
    return lax.broadcasted_iota(jnp.int32, shape, 1)


def turned(value, amount):
    amount = amount % value.shape[1]
    return value if amount == 0 else pltpu.roll(value, amount, 1)


def pack_pieces(still_ref, moving_ref, low_ref, high_ref, shifted_ref, piece_ref):
    depth = still_ref.shape[1]
    count = still_ref.shape[2]
    for place in range(5):
        shifted_ref[place, 0:1, :] = low_ref[place]
        shifted_ref[place, 1:depth, :] = moving_ref[place, 0 : depth - 1, :]
        shifted_ref[place + 5, depth - 1 : depth, :] = high_ref[place]
        shifted_ref[place + 5, 0 : depth - 1, :] = moving_ref[place + 5, 1:depth, :]

    def load(number, lanes):
        if number in still:
            return still_ref[still.index(number), :, lanes]
        return shifted_ref[x_order.index(number), :, lanes]

    small = lane_of((depth, LANES))
    wide = lane_of((depth, count)) % BS
    first = slice(0, LANES)
    last = slice(count - LANES, count)
    for piece, (chosen, lanes, begin) in enumerate(
        [(y_downward, first, 0), (y_upward, last, LANES - BS)]
    ):
        packed = jnp.zeros((depth, LANES), jnp.float32)
        for j in range(4):
            moved = turned(load(chosen[j], lanes), j * BS - begin)
            packed = jnp.where(small // BS == j, moved, packed)
        piece_ref[piece, :, 0:LANES] = packed
        piece_ref[piece, :, LANES:FACE] = turned(load(chosen[4], lanes), -begin)
    for piece, (chosen, begin) in enumerate([(z_downward, 0), (z_upward, BS - 1)]):
        gathered = jnp.zeros((depth, count), jnp.float32)
        for j in range(5):
            moved = turned(load(chosen[j], slice(0, count)), j - begin)
            gathered = jnp.where(wide == j, moved, gathered)
        for half in range(2):
            packed = jnp.zeros((depth, LANES), jnp.float32)
            for u in range(4):
                tile = half * 4 + u
                moved = turned(gathered[:, tile * LANES : (tile + 1) * LANES], 8 * u)
                packed = jnp.where(small % BS // 8 == u, moved, packed)
            piece_ref[2 + piece, :, half * LANES : (half + 1) * LANES] = packed
    for piece, (number, lanes) in enumerate([(16, first), (18, first), (17, last), (15, last)]):
        piece_ref[4 + piece, :, 0:LANES] = load(number, lanes)


def stream_into(still_ref, shifted_ref, message_ref, out_ref):
    depth = still_ref.shape[1]
    count = still_ref.shape[2]
    small = lane_of((depth, LANES))
    wide = lane_of((depth, count)) % BS
    columns = []
    for piece in range(2):
        tiles = []
        for half in range(2):
            packed = message_ref[2 + piece, :, half * LANES : (half + 1) * LANES]
            tiles += [turned(packed, -8 * u) for u in range(4)]
        columns.append(jnp.concatenate(tiles, axis=1))
    corners = {15: (4, 0, 127), 17: (5, 31, 96), 18: (6, 96, 31), 16: (7, 127, 0)}
    for number, (shift_x, shift_y, shift_z) in enumerate(velocity_list):
        if number in still:
            value = still_ref[still.index(number)]
        else:
            value = shifted_ref[x_order.index(number)]
        value = turned(value, shift_y * BS + shift_z)
        if shift_z != 0:
            chosen, piece, edge = (z_upward, 0, 0) if shift_z == 1 else (z_downward, 1, BS - 1)
            column = turned(columns[piece], edge - chosen.index(number) + BS * shift_y)
            value = jnp.where(wide == edge, column, value)
        out_ref[number] = value
        if shift_y != 0:
            chosen, piece, lanes, edge = (
                (y_upward, 0, slice(0, LANES), 0)
                if shift_y == 1
                else (y_downward, 1, slice(count - LANES, count), LANES - BS)
            )
            j = chosen.index(number)
            begin = j // 4 * LANES
            row = message_ref[piece, :, begin : begin + LANES]
            row = turned(row, edge - j % 4 * BS + shift_z)
            keep = small // BS == edge // BS
            if shift_z != 0:
                keep = keep & (small % BS != (0 if shift_z == 1 else BS - 1))
            old = value[:, lanes]
            fixed = jnp.where(keep, row, old)
            if number in corners:
                slot, lane_to, lane_from = corners[number]
                corner = turned(message_ref[slot, :, 0:LANES], lane_to - lane_from)
                fixed = jnp.where(small == lane_to, corner, fixed)
            out_ref[number, :, lanes] = fixed


def window_kernel(
    blocks, ring, target_ref, start_ref, field_ref, density_ref,
    still_ref, moving_ref, shifted_ref, up_ref, down_ref, low_ref, high_ref,
    piece_ref, send_ref, got_ref, edge_send, edge_got, send_sem, got_sem,
):
    mesh_ids = pl.DeviceIdType.MESH
    me = lax.axis_index("blk")
    side = lax.axis_index("obs")
    right = lax.rem(side + 1, ring)
    left = lax.rem(side + ring - 1, ring)
    barrier = pltpu.get_barrier_semaphore()

    def greet(distance, carry):
        peer = lax.rem(me + distance, blocks)
        pl.semaphore_signal(barrier, inc=1, device_id=(peer, side), device_id_type=mesh_ids)
        return carry

    for beside in (left, right):
        pl.semaphore_signal(barrier, inc=1, device_id=(me, beside), device_id_type=mesh_ids)
    lax.fori_loop(1, blocks, greet, 0)
    field_ref[...] = start_ref[...]
    pl.semaphore_wait(barrier, blocks + 1)

    def one_step(step, carry):
        collide_all(field_ref, still_ref, moving_ref, up_ref, down_ref)
        edges = [
            pltpu.make_async_remote_copy(
                src_ref=source,
                dst_ref=into.at[step],
                send_sem=edge_send.at[step, way],
                recv_sem=edge_got.at[step, way],
                device_id=(me, beside),
                device_id_type=mesh_ids,
            )
            for way, (source, into, beside) in enumerate(
                [(up_ref, low_ref, right), (down_ref, high_ref, left)]
            )
        ]
        for edge in edges:
            edge.start()
        for edge in edges:
            edge.wait()
        pack_pieces(
            still_ref, moving_ref, low_ref.at[step], high_ref.at[step], shifted_ref, piece_ref
        )

        def copy_to(distance):
            return pltpu.make_async_remote_copy(
                src_ref=send_ref.at[distance],
                dst_ref=got_ref.at[step, me],
                send_sem=send_sem.at[step, distance],
                recv_sem=got_sem.at[step, distance],
                device_id=(lax.rem(me + distance, blocks), side),
                device_id_type=mesh_ids,
            )

        def fill(distance, inner):
            peer = lax.rem(me + distance, blocks)
            near = jnp.zeros((send_ref.shape[1], LANES), jnp.float32)
            rest = near
            for piece in range(8):
                wanted = target_ref[piece] == peer
                near = jnp.where(wanted, piece_ref[piece, :, 0:LANES], near)
                if piece < 4:
                    rest = jnp.where(wanted, piece_ref[piece, :, LANES:FACE], rest)
            send_ref[distance, :, 0:LANES] = near
            send_ref[distance, :, LANES:FACE] = rest
            return inner

        def begin(distance, inner):
            copy_to(distance).start()
            return inner

        def finish(distance, inner):
            copy_to(distance).wait()
            return inner

        lax.fori_loop(1, blocks, fill, 0)
        lax.fori_loop(1, blocks, begin, 0)
        lax.fori_loop(1, blocks, finish, 0)

        def choose(distance, held):
            peer = lax.rem(me + distance, blocks)
            near = got_ref[step, peer, :, 0:LANES]
            rest = got_ref[step, peer, :, LANES:FACE]
            wanted = [target_ref[piece] == peer for piece in range(8)]
            return tuple(
                jnp.where(wanted[at % 8], near if at < 8 else rest, held[at]) for at in range(12)
            )

        blank = jnp.zeros((send_ref.shape[1], LANES), jnp.float32)
        held = lax.fori_loop(1, blocks, choose, (blank,) * 12)
        for at in range(12):
            half = at // 8 * LANES
            piece_ref[at % 8, :, half : half + LANES] = held[at]
        stream_into(still_ref, shifted_ref, piece_ref, field_ref)
        total = field_ref[0]
        for number in range(1, 19):
            total = total + field_ref[number]
        density_ref[step] = total
        return carry

    lax.fori_loop(0, STEPS, one_step, 0)


def call(kernel, outs, scalars, *arrays, scratch=()):
    vmem = pl.BlockSpec(memory_space=pltpu.VMEM)
    smem = pl.BlockSpec(memory_space=pltpu.SMEM)
    shapes = [jax.ShapeDtypeStruct(shape, jnp.float32) for shape in outs]
    return pl.pallas_call(
        kernel,
        out_shape=shapes,
        in_specs=[smem] * len(scalars) + [vmem] * len(arrays),
        out_specs=[vmem] * len(outs),
        scratch_shapes=[pltpu.VMEM(shape, jnp.float32) for shape in scratch],
    )(*scalars, *arrays)


def transform_table():
    moments = jnp.arange(SAMPLES, dtype=jnp.int32)[:, None]
    harmonics = jnp.arange(BINS, dtype=jnp.int32)[None, :] + 1
    turns = moments * harmonics % SAMPLES
    phases = turns.astype(jnp.float32) * (2.0 * math.pi / SAMPLES)
    return jnp.concatenate([jnp.cos(phases), -jnp.sin(phases)], axis=1).astype(jnp.bfloat16)


def greet_peers(blocks):
    me = lax.axis_index("blk")
    side = lax.axis_index("obs")
    barrier = pltpu.get_barrier_semaphore()

    def greet(distance, carry):
        pl.semaphore_signal(
            barrier, inc=1, device_id=(lax.rem(me + distance, blocks), side),
            device_id_type=pl.DeviceIdType.MESH,
        )
        return carry

    lax.fori_loop(1, blocks, greet, 0)
    return barrier


def swap_pieces(blocks, send_ref, got_ref, send_sem, got_sem):
    me = lax.axis_index("blk")
    side = lax.axis_index("obs")

    def copy_to(distance):
        peer = lax.rem(me + distance, blocks)
        return pltpu.make_async_remote_copy(
            src_ref=send_ref.at[peer],
            dst_ref=got_ref.at[me],
            send_sem=send_sem.at[distance],
            recv_sem=got_sem.at[distance],
            device_id=(peer, side),
            device_id_type=pl.DeviceIdType.MESH,
        )

    def begin(distance, inner):
        copy_to(distance).start()
        return inner

    def finish(distance, inner):
        copy_to(distance).wait()
        return inner

    lax.fori_loop(1, blocks, begin, 0)
    lax.fori_loop(1, blocks, finish, 0)


def exchange_kernel(blocks, source_ref, out_ref, got_ref, send_sem, got_sem):
    me = lax.axis_index("blk")
    barrier = greet_peers(blocks)
    got_ref[me] = source_ref[me]
    pl.semaphore_wait(barrier, blocks - 1)
    swap_pieces(blocks, source_ref, got_ref, send_sem, got_sem)
    out_ref[...] = got_ref[...]


def radiate_kernel(
    blocks, panel_ref, listen_ref, out_ref,
    real_ref, imag_ref, full_ref, send_ref, got_ref, send_sem, got_sem,
):
    barrier = greet_peers(blocks)
    listeners = listen_ref.shape[1]
    real_ref[...] = jnp.zeros_like(real_ref)
    imag_ref[...] = jnp.zeros_like(imag_ref)
    step_angle = 2.0 * math.pi / SAMPLES / sound_speed

    def accumulate(block_number, carry):
        begin = pl.multiple_of(block_number * 8, 8)
        panel = panel_ref[pl.ds(begin, 8), :]
        distance_sq = None
        facing = None
        for axis in range(3):
            at = 4 * BINS + axis
            offset = listen_ref[axis : axis + 1, :] - panel[:, at : at + 1]
            square = offset * offset
            along = panel[:, at + 3 : at + 4] * offset
            distance_sq = square if distance_sq is None else distance_sq + square
            facing = along if facing is None else facing + along
        distance = jnp.sqrt(distance_sq)
        far_term = facing / (4.0 * math.pi * sound_speed * distance_sq)
        ratio = sound_speed / distance
        angle = step_angle * distance
        turn_cos = jnp.cos(angle)
        turn_sin = jnp.sin(angle)
        wave_cos = far_term * turn_cos
        wave_sin = far_term * turn_sin
        for k in range(BINS):
            press_real = panel[:, k : k + 1]
            press_imag = panel[:, BINS + k : BINS + k + 1]
            rate_real = panel[:, 2 * BINS + k : 2 * BINS + k + 1]
            rate_imag = panel[:, 3 * BINS + k : 3 * BINS + k + 1]
            mixed_real = rate_real + ratio * press_real
            mixed_imag = rate_imag + ratio * press_imag
            real_ref[k] += mixed_real * wave_cos + mixed_imag * wave_sin
            imag_ref[k] += mixed_imag * wave_cos - mixed_real * wave_sin
            if k + 1 < BINS:
                wave_cos, wave_sin = (
                    wave_cos * turn_cos - wave_sin * turn_sin,
                    wave_sin * turn_cos + wave_cos * turn_sin,
                )
        return carry

    lax.fori_loop(0, panel_ref.shape[0] // 8, accumulate, 0)
    both = jnp.concatenate([jnp.sum(real_ref[...], axis=1), jnp.sum(imag_ref[...], axis=1)], axis=0)
    full_ref[...] = both.T
    chunk = out_ref.shape[0]
    for number in range(blocks):
        send_ref[number] = full_ref[number * chunk : (number + 1) * chunk]
    me = lax.axis_index("blk")
    got_ref[me] = send_ref[me]
    pl.semaphore_wait(barrier, blocks - 1)
    swap_pieces(blocks, send_ref, got_ref, send_sem, got_sem)
    out_ref[...] = jnp.sum(got_ref[...], axis=0)


def route_slots(payload, owners, alive_slot, blocks):
    count_slots = payload.shape[0]
    capacity = -(-count_slots // blocks)
    target = owners // P_OWN
    member = (
        (target[:, None] == jnp.arange(blocks, dtype=jnp.int32)[None, :]) & alive_slot[:, None]
    ).astype(jnp.int32)
    before = jnp.cumsum(member, axis=0) - member
    order_within = jnp.sum(before * member, axis=1)
    slot_label = jnp.where(alive_slot, target * capacity + order_within, -1)
    matches = slot_label[:, None] == jnp.arange(blocks * capacity, dtype=jnp.int32)[None, :]
    source = jnp.sum(
        jnp.where(matches, jnp.arange(count_slots, dtype=jnp.int32)[:, None], 0), axis=0
    )
    filled = jnp.any(matches, axis=0)
    outgoing = jnp.take(payload, source, axis=0).reshape(blocks, capacity, payload.shape[1])
    spots = jnp.where(filled, jnp.take(owners, source) % P_OWN, -1).reshape(blocks, capacity, 1)
    return jnp.concatenate([outgoing, spots.astype(jnp.bfloat16)], axis=2)


def settle(incoming):
    width = incoming.shape[-1] - 1
    flat = incoming.reshape(-1, width + 1)
    spots = flat[:, width].astype(jnp.int32)
    choose = (spots[:, None] == jnp.arange(P_OWN, dtype=jnp.int32)[None, :]).astype(jnp.bfloat16)
    return jnp.einsum(
        "rp,rw->pw", choose, flat[:, :width], preferred_element_type=jnp.float32
    ).astype(jnp.bfloat16)


def body(
    populations,
    block_faces,
    block_edges,
    probe_cell,
    history,
    panel_count,
    panel_owner,
    panel_pos,
    panel_normal,
    observers,
):
    blocks = lax.axis_size("blk")
    lattice_state = populations[0]
    slab_depth = lattice_state.shape[1]
    lane_count = lattice_state.shape[2]
    targets = jnp.concatenate([block_faces[0], block_edges[0]])
    ring = lax.axis_size("obs")
    still_shape = (len(still), slab_depth, lane_count)
    moving_shape = (len(x_order), slab_depth, lane_count)
    edge_shape = (5, 1, lane_count)
    vmem = pl.BlockSpec(memory_space=pltpu.VMEM)
    scratch = [
        still_shape, moving_shape, moving_shape, edge_shape, edge_shape,
        (STEPS,) + edge_shape, (STEPS,) + edge_shape,
        (8, slab_depth, FACE), (blocks, slab_depth, FACE), (STEPS, blocks, slab_depth, FACE),
    ]
    lattice_state, densities = pl.pallas_call(
        functools.partial(window_kernel, blocks, ring),
        out_shape=[
            jax.ShapeDtypeStruct((19, slab_depth, lane_count), jnp.float32),
            jax.ShapeDtypeStruct((STEPS, slab_depth, lane_count), jnp.float32),
        ],
        in_specs=[pl.BlockSpec(memory_space=pltpu.SMEM), vmem],
        out_specs=[vmem, vmem],
        scratch_shapes=[pltpu.VMEM(shape, jnp.float32) for shape in scratch]
        + [pltpu.SemaphoreType.DMA((STEPS, 2))] * 2
        + [pltpu.SemaphoreType.DMA((STEPS, blocks))] * 2,
        compiler_params=pltpu.CompilerParams(collective_id=0, has_side_effects=True),
    )(targets, lattice_state)
    populations_out = lattice_state.reshape(1, 19, slab_depth, lane_count)
    readings = [jnp.take(density.reshape(-1), probe_cell) for density in densities]
    gained = pressure_gain * (jnp.stack(readings, axis=1) - 1.0)
    previous = jnp.concatenate(
        [history[:, SAMPLES - 1 : SAMPLES].astype(jnp.float32), gained[:, :-1]], axis=1
    )
    rate_values = gained - previous
    recent = jnp.concatenate(
        [
            history[:, STEPS:SAMPLES],
            gained.astype(jnp.bfloat16),
            history[:, SAMPLES + STEPS :],
            rate_values.astype(jnp.bfloat16),
        ],
        axis=1,
    )
    transform = transform_table()
    count_slots = recent.shape[0]
    alive_slot = jnp.arange(count_slots, dtype=jnp.int32) < panel_count[0]
    outgoing = route_slots(recent, panel_owner, alive_slot, blocks)
    incoming = pl.pallas_call(
        functools.partial(exchange_kernel, blocks),
        out_shape=jax.ShapeDtypeStruct(outgoing.shape, outgoing.dtype),
        in_specs=[vmem],
        out_specs=vmem,
        scratch_shapes=[pltpu.VMEM(outgoing.shape, outgoing.dtype)]
        + [pltpu.SemaphoreType.DMA((blocks,))] * 2,
        compiler_params=pltpu.CompilerParams(collective_id=1, has_side_effects=True),
    )(outgoing)
    owned = settle(incoming).reshape(P_OWN, 2, SAMPLES)
    spectra = (
        jnp.einsum("pgt,tk->pgk", owned, transform, preferred_element_type=jnp.float32)
        .astype(jnp.bfloat16)
        .reshape(P_OWN, 4 * BINS)
    )
    panels = jnp.concatenate([spectra, panel_pos.T, panel_normal.T], axis=1)
    gathered = lax.all_gather(panels, "obs", axis=0, tiled=True).astype(jnp.float32)
    listeners = observers.shape[1]
    chunk = listeners // blocks
    spectrum = pl.pallas_call(
        functools.partial(radiate_kernel, blocks),
        out_shape=jax.ShapeDtypeStruct((chunk, 2 * BINS), jnp.float32),
        in_specs=[vmem, vmem],
        out_specs=vmem,
        scratch_shapes=[
            pltpu.VMEM(shape, jnp.float32)
            for shape in [
                (BINS, 8, listeners), (BINS, 8, listeners), (listeners, 2 * BINS),
                (blocks, chunk, 2 * BINS), (blocks, chunk, 2 * BINS),
            ]
        ]
        + [pltpu.SemaphoreType.DMA((blocks,))] * 2,
        compiler_params=pltpu.CompilerParams(collective_id=2, has_side_effects=True),
    )(gathered, observers)
    return (populations_out, spectrum[None])


def solution(mesh):
    placed = (
        P("blk", None, "obs", None),
        P("blk", None),
        P("blk", None),
        P(("blk", "obs")),
        P(("blk", "obs"), None),
        P(("blk", "obs")),
        P(("blk", "obs")),
        P(None, ("blk", "obs")),
        P(None, ("blk", "obs")),
        P(None, "obs"),
    )
    return jax.shard_map(
        body,
        mesh=mesh,
        in_specs=placed,
        out_specs=(P("blk", None, "obs", None), P("obs", "blk", None)),
        check_vma=False,
    )
```

profile of v0, /device:TPU:0, one launch (start us, length us, event | category | flops | bytes accessed | tf_op | source)
XLA Modules:
  0.0 108.3 jit_solution(14546182929525627522)
XLA Ops:
  0.6 1.3 %pad_add_fusion.target_ref = s32[8]{0:T(128)} fusion(s32[4]{0:T(128)} %bitcast.67, s32[4]{0:T(128)} %bitcast.68), kind=kLoop, calls=%fused_computation.67 | loop fusion | flops 8 | bytes 64 | tf_op jit(solution)/shard_map/concatenate | solution.py:498
  1.9 53.8 %shard_map.113 = (f32[19,16,1024]{2,1,0:T(8,128)}, f32[4,16,1024]{2,1,0:T(8,128)}) custom-call(s32[8]{0:T(128)} %pad_add_fusion.target_ref, f32[19,16,1024]{2,1,0:T(8,128)} %bitcast.57), custom_call_target="tpu_custom_call" | custom-call | tf_op jit(solution)/shard_map/pallas_call | solution.py:509
  55.7 1.0 slice_bitcast_fusion.2
  56.7 1.1 %gather_fusion.2 = f32[128]{0:T(128)S(1)} fusion(f32[16384]{0:T(1024)S(1)} %bitcast.53, s32[1024]{0:T(1024)S(1)} %pad_clamp_fusion.1), kind=kCustom, calls=%fused_computation.clone | custom fusion | bytes 1536 | tf_op jit(solution)/shard_map/jit(_take)/gather | solution.py:523
  57.9 1.1 %gather_fusion.3 = f32[128]{0:T(128)S(1)} fusion(f32[16384]{0:T(1024)S(1)} %bitcast.55, s32[1024]{0:T(1024)S(1)} %pad_clamp_fusion.1), kind=kCustom, calls=%fused_computation.1.clone | custom fusion | bytes 1536 | tf_op jit(solution)/shard_map/jit(_take)/gather | solution.py:523
  59.1 1.1 %gather_fusion.4 = f32[128]{0:T(128)S(1)} fusion(f32[16384]{0:T(1024)S(1)} %bitcast.56, s32[1024]{0:T(1024)S(1)} %pad_clamp_fusion.1), kind=kCustom, calls=%fused_computation.2.clone | custom fusion | bytes 1536 | tf_op jit(solution)/shard_map/jit(_take)/gather | solution.py:523
  60.3 1.1 %gather_fusion.5 = f32[128]{0:T(128)S(1)} fusion(f32[16384]{0:T(1024)S(1)} %bitcast.54, s32[1024]{0:T(1024)S(1)} %pad_clamp_fusion.1), kind=kCustom, calls=%fused_computation.3.clone | custom fusion | bytes 1536 | tf_op jit(solution)/shard_map/jit(_take)/gather | solution.py:523
  63.0 0.2 reduce_window_sum.11
  63.1 0.2 select_reduce_fusion.1
  63.5 0.8 gather_fusion
  64.5 1.2 %gather_fusion.1 = s32[128]{0:T(128)S(1)} fusion(s32[128]{0:T(128)S(1)} %copy-done, s32[1024]{0:T(1024)S(1)} %pad_clamp_fusion), kind=kCustom, calls=%fused_computation.5 | custom fusion | bytes 1536 | tf_op jit(solution)/shard_map/jit(_take)/gather | solution.py:468
  65.8 0.2 gather.38
  66.0 0.2 reduce_sum.29
  66.3 0.2 reduce_or.13
  66.6 0.7 pad_maximum_fusion.source_ref
  67.3 10.7 %shard_map.114 = bf16[16,8,513]{2,1,0:T(8,128)(2,1)} custom-call(bf16[16,8,513]{2,1,0:T(8,128)(2,1)} %pad_maximum_fusion.source_ref), custom_call_target="tpu_custom_call" | custom-call | tf_op jit(solution)/shard_map/pallas_call | solution.py:542
  77.9 0.8 slice.36
  78.8 1.2 %convolution_convert_fusion = bf16[64,512]{1,0:T(8,128)(2,1)S(1)} fusion(bf16[128,513]{1,0:T(8,128)(2,1)} %bitcast.60, s32[128]{0:T(128)S(1)} %bitcast_convert_fusion), kind=kOutput, calls=%fused_computation.6 | convolution fusion | flops 8429568 | bytes 197120 | tf_op jit(solution)/shard_map/rp,rw->pw/dot_general | solution.py:477
  80.0 0.3 cosine_convert_fusion
  80.9 1.9 %all_gather.3 = bf16[128,262]{1,0:T(8,128)(2,1)S(1)} all-gather(bf16[64,262]{1,0:T(8,128)(2,1)S(1)} %pad_maximum_fusion.2), channel_id=1, replica_groups=mesh['blk'=16,'obs'=2] {'obs'}, dimensions={0}, use_global_device_ids=true | all-gather | bytes 100608 | tf_op jit(solution)/shard_map/all_gather | solution.py:558
  82.7 0.7 convert_element_type.49.panel_ref
  83.4 23.3 %shard_map.115 = f32[32,128]{1,0:T(8,128)} custom-call(f32[128,262]{1,0:T(8,128)} %convert_element_type.49.panel_ref, f32[3,512]{1,0:T(4,128)} %listen_ref.1), custom_call_target="tpu_custom_call" | custom-call | tf_op jit(solution)/shard_map/pallas_call | solution.py:561
  106.7 1.0 copy.103
  107.7 0.6 copy.104
  (51 shorter events, 2.0 us)
Async XLA Ops:
  0.6 56.0 %copy-start.6 = (s32[128]{0:T(128)S(1)}, s32[128]{0:T(128)}, u32[]{:S(2)}) copy-start(s32[128]{0:T(128)} %param.15) | copy-start | bytes 1540
  56.7 4.8 %copy-start.2 = (bf16[128,512]{1,0:T(8,128)(2,1)S(1)}, bf16[128,512]{1,0:T(8,128)(2,1)}, u32[]{:S(2)}) copy-start(bf16[128,512]{1,0:T(8,128)(2,1)} %param.16) | copy-start | bytes 393220
  57.9 4.9 %copy-start = (s32[128]{0:T(128)S(1)}, s32[128]{0:T(128)}, u32[]{:S(2)}) copy-start(s32[128]{0:T(128)} %param.18) | copy-start | bytes 1540
  64.3 16.2 %copy-start.4 = (bf16[3,64]{1,0:T(4,128)(2,1)S(1)}, bf16[3,64]{1,0:T(4,128)(2,1)}, u32[]{:S(2)}) copy-start(bf16[3,64]{1,0:T(4,128)(2,1)} %param.19) | copy-start | bytes 1156
  64.3 16.3 %copy-start.5 = (bf16[3,64]{1,0:T(4,128)(2,1)S(1)}, bf16[3,64]{1,0:T(4,128)(2,1)}, u32[]{:S(2)}) copy-start(bf16[3,64]{1,0:T(4,128)(2,1)} %param.20) | copy-start | bytes 1156
  65.8 40.9 %copy-start.1 = (f32[19,16,1024]{2,1,0:T(8,128)S(1)}, f32[19,16,1024]{2,1,0:T(8,128)}, u32[]{:S(2)}) copy-start(f32[19,16,1024]{2,1,0:T(8,128)} %get-tuple-element.5) | copy-start | bytes 3735556
  106.7 1.1 copy-start.3
where the time goes:
time: 109 us; the launch traced here: 108 us
  Pallas kernels  87.7 us (80%)
  local copies, waits for them, and re-layouts  11.7 us (11%)
  other arithmetic  4.12 us (4%)
  blocking collectives  1.87 us (2%)
  between operations  1.64 us (2%)
  matrix products  1.35 us (1%)
    pallas_call x1, Pallas kernels, body(): pl.pallas_call(functools.partial(window_kernel, blocks, ring), out_shape=...  53.8 us
    pallas_call x1, Pallas kernels, body(): pl.pallas_call(functools.partial(radiate_kernel, blocks), out_shape=jax.S...  23.3 us
    pallas_call x1, Pallas kernels, body(): pl.pallas_call(functools.partial(exchange_kernel, blocks), out_shape=jax....  10.7 us
    gather x4, local copies, waits for them, and re-layouts, body(): jnp.take(density.reshape(-1), probe_cell)  4.59 us
    unnamed x25, local copies, waits for them, and re-layouts  3.07 us

commit v1 on v0

v1 whole, which is shorter than its diff:
```python
import functools
import math

import jax
import jax.numpy as jnp
from jax import lax
from jax.experimental import pallas as pl
from jax.experimental.pallas import tpu as pltpu
from jax.sharding import PartitionSpec as P

BS = 32
STEPS = 4
SAMPLES = 256
BINS = 64
P_OWN = 64


velocity_list = [
    (0, 0, 0),
    (1, 0, 0),
    (-1, 0, 0),
    (0, 1, 0),
    (0, -1, 0),
    (0, 0, 1),
    (0, 0, -1),
    (1, 1, 0),
    (-1, -1, 0),
    (1, -1, 0),
    (-1, 1, 0),
    (1, 0, 1),
    (-1, 0, -1),
    (1, 0, -1),
    (-1, 0, 1),
    (0, 1, 1),
    (0, -1, -1),
    (0, 1, -1),
    (0, -1, 1),
]
weight_list = [1.0 / 3.0] + [1.0 / 18.0] * 6 + [1.0 / 36.0] * 12
x_moving = [1, 2, 7, 8, 9, 10, 11, 12, 13, 14]
y_upward = [3, 7, 10, 15, 17]
y_downward = [4, 8, 9, 16, 18]
z_upward = [5, 11, 14, 15, 18]
z_downward = [6, 12, 13, 16, 17]
relax_rate = 1.6
pressure_gain = 60.0
sound_speed = 0.5


x_plus = [1, 7, 9, 11, 13]
x_minus = [2, 8, 10, 12, 14]
x_order = x_plus + x_minus
still = [0, 3, 4, 5, 6, 15, 16, 17, 18]
LANES = 128
FACE = 256


def collide_tile(f):
    sums = [None] * 19
    gaps = [None] * 19
    for number in range(1, 19, 2):
        sums[number] = f[number] + f[number + 1]
        gaps[number] = f[number] - f[number + 1]
    density = f[0]
    for number in range(1, 19, 2):
        density = density + sums[number]
    speeds = []
    for axis in range(3):
        total = None
        for number in range(1, 19, 2):
            sign = velocity_list[number][axis]
            if sign == 0:
                continue
            if total is None:
                total = gaps[number]
            elif sign == 1:
                total = total + gaps[number]
            else:
                total = total - gaps[number]
        speeds.append(total)
    inverse = 1.0 / density
    speeds = [speed * inverse for speed in speeds]
    squared = speeds[0] * speeds[0] + speeds[1] * speeds[1] + speeds[2] * speeds[2]
    base = 1.0 - 1.5 * squared
    keep = 1.0 - relax_rate
    out = [None] * 19
    out[0] = keep * f[0] + ((relax_rate * weight_list[0]) * density) * base
    scaled = {}
    thrice = {}
    for weight in sorted(set(weight_list[1:])):
        scaled[weight] = (relax_rate * weight) * density
        thrice[weight] = 3.0 * scaled[weight]
    for number in range(1, 19, 2):
        projected = None
        for axis in range(3):
            sign = velocity_list[number][axis]
            if sign == 0:
                continue
            if projected is None:
                projected = speeds[axis]
            elif sign == 1:
                projected = projected + speeds[axis]
            else:
                projected = projected - speeds[axis]
        weight = weight_list[number]
        even = scaled[weight] * (base + 4.5 * (projected * projected))
        odd = thrice[weight] * projected
        out[number] = keep * f[number] + (even + odd)
        out[number + 1] = keep * f[number + 1] + (even - odd)
    return out


def lane_of(shape):
    return lax.broadcasted_iota(jnp.int32, shape, 1)


def turned(value, amount):
    amount = amount % value.shape[1]
    return value if amount == 0 else pltpu.roll(value, amount, 1)


def pushed(value, low, high, sign):
    if sign == 1:
        return jnp.concatenate([low, value[:-1]], axis=0)
    return jnp.concatenate([value[1:], high], axis=0)


def shift_of(number):
    return velocity_list[number][1] * BS + velocity_list[number][2]


face_sets = [y_downward, y_upward, z_downward, z_upward]


def collide_all(field_ref, rolled_ref, moving_ref, edge_ref, piece_ref, rim_ref):
    depth = field_ref.shape[1]
    tiles = field_ref.shape[2] // LANES
    spot = lane_of((depth, LANES)) % BS
    quarter = lane_of((depth, LANES)) // BS
    for half in range(tiles // 4):
        packed = [jnp.zeros((depth, LANES), jnp.float32) for piece in range(2)]
        for u in range(4):
            tile = half * 4 + u
            lanes = slice(tile * LANES, (tile + 1) * LANES)
            out = collide_tile([field_ref[number, :, lanes] for number in range(19)])
            for number in range(19):
                if number in still:
                    rolled_ref[tile + 1, number] = turned(out[number], shift_of(number))
                else:
                    moving_ref[tile, x_order.index(number)] = out[number]
            for place, number in enumerate(x_plus):
                edge_ref[0, place, tile : tile + 1, :] = out[number][depth - 1 : depth]
            for place, number in enumerate(x_minus):
                edge_ref[1, place, tile : tile + 1, :] = out[number][0:1]
            for side, (chosen, begin) in enumerate([(z_downward, 0), (z_upward, BS - 1)]):
                for j, number in enumerate(chosen):
                    moved = turned(out[number] - weight_list[number], 8 * u + j - begin)
                    packed[side] = jnp.where(spot == 8 * u + j, moved, packed[side])
            for side, (chosen, at, begin) in enumerate(
                [(y_downward, 0, 0), (y_upward, tiles - 1, LANES - BS)]
            ):
                if tile != at:
                    continue
                values = [out[number] - weight_list[number] for number in chosen]
                row = jnp.zeros((depth, LANES), jnp.float32)
                for j in range(4):
                    row = jnp.where(quarter == j, turned(values[j], j * BS - begin), row)
                store_piece(piece_ref, rim_ref, side, 0, row)
                store_piece(piece_ref, rim_ref, side, 1, turned(values[4], -begin))
        for side in range(2):
            store_piece(piece_ref, rim_ref, 2 + side, half, packed[side])


def store_piece(piece_ref, rim_ref, piece, half, value):
    depth = value.shape[0]
    lanes = slice(half * LANES, (half + 1) * LANES)
    piece_ref[piece, :, lanes] = value.astype(jnp.bfloat16)
    rim_ref[piece, 0, :, lanes] = value[depth - 1 : depth]
    rim_ref[piece, 1, :, lanes] = value[0:1]


def roll_moving(rolled_ref, moving_ref, near_ref):
    tiles = moving_ref.shape[0]
    for tile in range(tiles):
        for place, number in enumerate(x_order):
            low = near_ref[0, place % 5, tile : tile + 1, :]
            high = near_ref[1, place % 5, tile : tile + 1, :]
            value = pushed(moving_ref[tile, place], low, high, velocity_list[number][0])
            rolled_ref[tile + 1, number] = turned(value, shift_of(number))


def finish_step(face, edge, got_ref, rim_got_ref, rolled_ref, field_ref, density_ref):
    depth = field_ref.shape[1]
    tiles = field_ref.shape[2] // LANES
    lane = lane_of((depth, LANES))
    spot = lane % BS

    def arrived(piece, source, half):
        chosen = face_sets[piece]
        lanes = slice(half * LANES, (half + 1) * LANES)
        value = got_ref[source, :, lanes].astype(jnp.float32)
        low = rim_got_ref[source, 0, :, lanes]
        high = rim_got_ref[source, 1, :, lanes]
        for j, number in enumerate(chosen):
            sign = velocity_list[number][0]
            if sign == 0:
                continue
            if piece < 2:
                if j // 4 != half:
                    continue
                wanted = lane // BS == j % 4
            else:
                wanted = lane % 8 == j
            base = got_ref[source, :, lanes].astype(jnp.float32)
            value = jnp.where(wanted, pushed(base, low, high, sign), value)
        return value

    corners = {15: (0, 0, 1), 17: (1, 1, 31), 18: (2, 1, 65), 16: (3, 0, 31)}
    corner_lane = {15: 0, 17: BS - 1, 18: LANES - BS, 16: LANES - 1}
    for piece, source, pad, begin in [(1, face[0], 0, 0), (0, face[1], tiles + 1, LANES - BS)]:
        halves = [arrived(piece, source, half) for half in range(2)]
        for j, number in enumerate(face_sets[piece]):
            shift_z = velocity_list[number][2]
            value = turned(halves[j // 4], begin + shift_z - j % 4 * BS)
            if number in corners:
                which, half, amount = corners[number]
                lanes = slice(half * LANES, (half + 1) * LANES)
                corner = turned(got_ref[edge[which], :, lanes].astype(jnp.float32), amount)
                value = jnp.where(lane == corner_lane[number], corner, value)
            rolled_ref[pad, number] = value + weight_list[number]
    columns = {}
    for piece, source, rim in [(3, face[2], 0), (2, face[3], BS - 1)]:
        chosen = face_sets[piece]
        halves = [arrived(piece, source, half) for half in range(2)]
        for tile in range(tiles):
            for j, number in enumerate(chosen):
                shift_y = velocity_list[number][1]
                amount = rim - 8 * (tile % 4) - j + BS * shift_y
                column = turned(halves[tile // 4], amount) + weight_list[number]
                value = jnp.where(spot == rim, column, rolled_ref[tile + 1, number])
                if shift_y != 0:
                    rolled_ref[tile + 1, number] = value
                else:
                    columns[tile, number] = value
                    field_ref[number, :, tile * LANES : (tile + 1) * LANES] = value
    for tile in range(tiles):
        lanes = slice(tile * LANES, (tile + 1) * LANES)
        total = None
        for number, (_, shift_y, shift_z) in enumerate(velocity_list):
            if shift_y == 0 and shift_z != 0:
                value = field_ref[number, :, lanes]
            else:
                value = rolled_ref[tile + 1, number]
                if shift_y == 1:
                    value = jnp.where(lane < BS, rolled_ref[tile, number], value)
                elif shift_y == -1:
                    value = jnp.where(lane >= LANES - BS, rolled_ref[tile + 2, number], value)
                field_ref[number, :, lanes] = value
            total = value if total is None else total + value
        density_ref[:, lanes] = total


def window_kernel(
    blocks, ring, face_ref, rim_face_ref, start_ref, field_ref, density_ref,
    rolled_ref, moving_ref, edge_ref, near_ref, piece_ref, rim_ref,
    send_ref, got_even, got_odd, rim_send_ref, rim_got_even, rim_got_odd,
    edge_send, edge_got, send_sem, got_sem, rim_send_sem, rim_got_sem,
):
    mesh_ids = pl.DeviceIdType.MESH
    me = lax.axis_index("blk")
    side = lax.axis_index("obs")
    right = lax.rem(side + 1, ring)
    left = lax.rem(side + ring - 1, ring)
    sides = [side, right] if ring == 2 else [side, right, left]
    barrier = pltpu.get_barrier_semaphore()

    def greet(distance, carry):
        peer = lax.rem(me + distance, blocks)
        for other in sides:
            pl.semaphore_signal(barrier, inc=1, device_id=(peer, other), device_id_type=mesh_ids)
        return carry

    for beside in sides[1:]:
        pl.semaphore_signal(barrier, inc=1, device_id=(me, beside), device_id_type=mesh_ids)
    lax.fori_loop(1, blocks, greet, 0)
    face = [face_ref[0, k] for k in range(4)]
    edge = [rim_face_ref[0, k] for k in range(4)]
    field_ref[...] = start_ref[...]

    def one_step(step, got_ref, rim_got_ref):
        collide_all(field_ref, rolled_ref, moving_ref, edge_ref, piece_ref, rim_ref)

        if rim_got_ref is rim_got_even:

            @pl.when(step == 0)
            def _():
                pl.semaphore_wait(barrier, len(sides) * blocks - 1)

        edges = [
            pltpu.make_async_remote_copy(
                src_ref=edge_ref.at[way],
                dst_ref=near_ref.at[step, way],
                send_sem=edge_send.at[step, way],
                recv_sem=edge_got.at[step, way],
                device_id=(me, beside),
                device_id_type=mesh_ids,
            )
            for way, beside in enumerate([right, left])
        ]
        for copy in edges:
            copy.start()

        def copies_to(distance):
            peer = lax.rem(me + distance, blocks)
            copies = [
                pltpu.make_async_remote_copy(
                    src_ref=send_ref.at[distance],
                    dst_ref=got_ref.at[me],
                    send_sem=send_sem.at[step, distance],
                    recv_sem=got_sem.at[step, distance],
                    device_id=(peer, side),
                    device_id_type=mesh_ids,
                )
            ]
            if ring == 2:
                copies.append(
                    pltpu.make_async_remote_copy(
                        src_ref=rim_send_ref.at[distance],
                        dst_ref=rim_got_ref.at[me],
                        send_sem=rim_send_sem.at[step, distance, 0],
                        recv_sem=rim_got_sem.at[step, distance, 0],
                        device_id=(peer, right),
                        device_id_type=mesh_ids,
                    )
                )
            else:
                for way, other in enumerate([right, left]):
                    copies.append(
                        pltpu.make_async_remote_copy(
                            src_ref=rim_send_ref.at[distance, way],
                            dst_ref=rim_got_ref.at[me, way],
                            send_sem=rim_send_sem.at[step, distance, way],
                            recv_sem=rim_got_sem.at[step, distance, way],
                            device_id=(peer, other),
                            device_id_type=mesh_ids,
                        )
                    )
            return copies

        def begin(distance, inner):
            peer = lax.rem(me + distance, blocks)
            up = (peer == face[1]) | (peer == edge[2]) | (peer == edge[3])
            piece = jnp.where(peer == face[3], 3, jnp.where(peer == face[2], 2, up.astype(jnp.int32)))
            send_ref[distance] = piece_ref[piece]
            rim_send_ref[distance] = rim_ref[piece]
            for copy in copies_to(distance):
                copy.start()
            return inner

        def finish(distance, inner):
            for copy in copies_to(distance):
                copy.wait()
            return inner

        lax.fori_loop(1, blocks, begin, 0)
        for copy in edges:
            copy.wait()
        roll_moving(rolled_ref, moving_ref, near_ref.at[step])
        lax.fori_loop(1, blocks, finish, 0)
        finish_step(
            face, edge, got_ref, rim_got_ref,
            rolled_ref, field_ref, density_ref.at[step],
        )

    def two_steps(turn, carry):
        one_step(turn * 2, got_even, rim_got_even)
        one_step(turn * 2 + 1, got_odd, rim_got_odd)
        return carry

    lax.fori_loop(0, STEPS // 2, two_steps, 0)


def call(kernel, outs, scalars, *arrays, scratch=()):
    vmem = pl.BlockSpec(memory_space=pltpu.VMEM)
    smem = pl.BlockSpec(memory_space=pltpu.SMEM)
    shapes = [jax.ShapeDtypeStruct(shape, jnp.float32) for shape in outs]
    return pl.pallas_call(
        kernel,
        out_shape=shapes,
        in_specs=[smem] * len(scalars) + [vmem] * len(arrays),
        out_specs=[vmem] * len(outs),
        scratch_shapes=[pltpu.VMEM(shape, jnp.float32) for shape in scratch],
    )(*scalars, *arrays)


def transform_table():
    moments = jnp.arange(SAMPLES, dtype=jnp.int32)[:, None]
    harmonics = jnp.arange(BINS, dtype=jnp.int32)[None, :] + 1
    turns = moments * harmonics % SAMPLES
    phases = turns.astype(jnp.float32) * (2.0 * math.pi / SAMPLES)
    return jnp.concatenate([jnp.cos(phases), -jnp.sin(phases)], axis=1).astype(jnp.bfloat16)


def greet_peers(blocks):
    me = lax.axis_index("blk")
    side = lax.axis_index("obs")
    barrier = pltpu.get_barrier_semaphore()

    def greet(distance, carry):
        pl.semaphore_signal(
            barrier, inc=1, device_id=(lax.rem(me + distance, blocks), side),
            device_id_type=pl.DeviceIdType.MESH,
        )
        return carry

    lax.fori_loop(1, blocks, greet, 0)
    return barrier


def swap_pieces(blocks, send_ref, got_ref, send_sem, got_sem):
    me = lax.axis_index("blk")
    side = lax.axis_index("obs")

    def copy_to(distance):
        peer = lax.rem(me + distance, blocks)
        return pltpu.make_async_remote_copy(
            src_ref=send_ref.at[peer],
            dst_ref=got_ref.at[me],
            send_sem=send_sem.at[distance],
            recv_sem=got_sem.at[distance],
            device_id=(peer, side),
            device_id_type=pl.DeviceIdType.MESH,
        )

    def begin(distance, inner):
        copy_to(distance).start()
        return inner

    def finish(distance, inner):
        copy_to(distance).wait()
        return inner

    lax.fori_loop(1, blocks, begin, 0)
    lax.fori_loop(1, blocks, finish, 0)


def exchange_kernel(blocks, source_ref, out_ref, got_ref, send_sem, got_sem):
    me = lax.axis_index("blk")
    barrier = greet_peers(blocks)
    got_ref[me] = source_ref[me]
    pl.semaphore_wait(barrier, blocks - 1)
    swap_pieces(blocks, source_ref, got_ref, send_sem, got_sem)
    out_ref[...] = got_ref[...]


def radiate_kernel(
    blocks, panel_ref, listen_ref, out_ref,
    real_ref, imag_ref, full_ref, send_ref, got_ref, send_sem, got_sem,
):
    barrier = greet_peers(blocks)
    listeners = listen_ref.shape[1]
    real_ref[...] = jnp.zeros_like(real_ref)
    imag_ref[...] = jnp.zeros_like(imag_ref)
    step_angle = 2.0 * math.pi / SAMPLES / sound_speed

    def accumulate(block_number, carry):
        begin = pl.multiple_of(block_number * 8, 8)
        panel = panel_ref[pl.ds(begin, 8), :]
        distance_sq = None
        facing = None
        for axis in range(3):
            at = 4 * BINS + axis
            offset = listen_ref[axis : axis + 1, :] - panel[:, at : at + 1]
            square = offset * offset
            along = panel[:, at + 3 : at + 4] * offset
            distance_sq = square if distance_sq is None else distance_sq + square
            facing = along if facing is None else facing + along
        distance = jnp.sqrt(distance_sq)
        far_term = facing / (4.0 * math.pi * sound_speed * distance_sq)
        ratio = sound_speed / distance
        angle = step_angle * distance
        turn_cos = jnp.cos(angle)
        turn_sin = jnp.sin(angle)
        wave_cos = far_term * turn_cos
        wave_sin = far_term * turn_sin
        for k in range(BINS):
            press_real = panel[:, k : k + 1]
            press_imag = panel[:, BINS + k : BINS + k + 1]
            rate_real = panel[:, 2 * BINS + k : 2 * BINS + k + 1]
            rate_imag = panel[:, 3 * BINS + k : 3 * BINS + k + 1]
            mixed_real = rate_real + ratio * press_real
            mixed_imag = rate_imag + ratio * press_imag
            real_ref[k] += mixed_real * wave_cos + mixed_imag * wave_sin
            imag_ref[k] += mixed_imag * wave_cos - mixed_real * wave_sin
            if k + 1 < BINS:
                wave_cos, wave_sin = (
                    wave_cos * turn_cos - wave_sin * turn_sin,
                    wave_sin * turn_cos + wave_cos * turn_sin,
                )
        return carry

    lax.fori_loop(0, panel_ref.shape[0] // 8, accumulate, 0)
    both = jnp.concatenate([jnp.sum(real_ref[...], axis=1), jnp.sum(imag_ref[...], axis=1)], axis=0)
    full_ref[...] = both.T
    chunk = out_ref.shape[0]
    for number in range(blocks):
        send_ref[number] = full_ref[number * chunk : (number + 1) * chunk]
    me = lax.axis_index("blk")
    got_ref[me] = send_ref[me]
    pl.semaphore_wait(barrier, blocks - 1)
    swap_pieces(blocks, send_ref, got_ref, send_sem, got_sem)
    out_ref[...] = jnp.sum(got_ref[...], axis=0)


def route_slots(payload, owners, alive_slot, blocks):
    count_slots = payload.shape[0]
    capacity = -(-count_slots // blocks)
    target = owners // P_OWN
    member = (
        (target[:, None] == jnp.arange(blocks, dtype=jnp.int32)[None, :]) & alive_slot[:, None]
    ).astype(jnp.int32)
    before = jnp.cumsum(member, axis=0) - member
    order_within = jnp.sum(before * member, axis=1)
    slot_label = jnp.where(alive_slot, target * capacity + order_within, -1)
    matches = slot_label[:, None] == jnp.arange(blocks * capacity, dtype=jnp.int32)[None, :]
    source = jnp.sum(
        jnp.where(matches, jnp.arange(count_slots, dtype=jnp.int32)[:, None], 0), axis=0
    )
    filled = jnp.any(matches, axis=0)
    outgoing = jnp.take(payload, source, axis=0).reshape(blocks, capacity, payload.shape[1])
    spots = jnp.where(filled, jnp.take(owners, source) % P_OWN, -1).reshape(blocks, capacity, 1)
    return jnp.concatenate([outgoing, spots.astype(jnp.bfloat16)], axis=2)


def settle(incoming):
    width = incoming.shape[-1] - 1
    flat = incoming.reshape(-1, width + 1)
    spots = flat[:, width].astype(jnp.int32)
    choose = (spots[:, None] == jnp.arange(P_OWN, dtype=jnp.int32)[None, :]).astype(jnp.bfloat16)
    return jnp.einsum(
        "rp,rw->pw", choose, flat[:, :width], preferred_element_type=jnp.float32
    ).astype(jnp.bfloat16)


def body(
    populations,
    block_faces,
    block_edges,
    probe_cell,
    history,
    panel_count,
    panel_owner,
    panel_pos,
    panel_normal,
    observers,
):
    blocks = lax.axis_size("blk")
    lattice_state = populations[0]
    slab_depth = lattice_state.shape[1]
    lane_count = lattice_state.shape[2]
    ring = lax.axis_size("obs")
    tiles = lane_count // LANES
    vmem = pl.BlockSpec(memory_space=pltpu.VMEM)
    smem = pl.BlockSpec(memory_space=pltpu.SMEM)
    wide = jnp.float32
    half = jnp.bfloat16
    lattice_state, densities = pl.pallas_call(
        functools.partial(window_kernel, blocks, ring),
        out_shape=[
            jax.ShapeDtypeStruct((19, slab_depth, lane_count), jnp.float32),
            jax.ShapeDtypeStruct((STEPS, slab_depth, lane_count), jnp.float32),
        ],
        in_specs=[smem, smem, vmem],
        out_specs=[vmem, vmem],
        scratch_shapes=[
            pltpu.VMEM((tiles + 2, 19, slab_depth, LANES), wide),
            pltpu.VMEM((tiles, len(x_order), slab_depth, LANES), wide),
            pltpu.VMEM((2, 5, tiles, LANES), wide),
            pltpu.VMEM((STEPS, 2, 5, tiles, LANES), wide),
            pltpu.VMEM((4, slab_depth, FACE), half),
            pltpu.VMEM((4, 2, 1, FACE), wide),
            pltpu.VMEM((blocks, slab_depth, FACE), half),
            pltpu.VMEM((blocks, slab_depth, FACE), half),
            pltpu.VMEM((blocks, slab_depth, FACE), half),
            pltpu.VMEM((blocks, 2, 1, FACE), wide),
            pltpu.VMEM((blocks, 2, 1, FACE), wide),
            pltpu.VMEM((blocks, 2, 1, FACE), wide),
        ]
        + [pltpu.SemaphoreType.DMA((STEPS, 2))] * 2
        + [pltpu.SemaphoreType.DMA((STEPS, blocks))] * 2
        + [pltpu.SemaphoreType.DMA((STEPS, blocks, 2))] * 2,
        compiler_params=pltpu.CompilerParams(collective_id=0, has_side_effects=True),
    )(block_faces, block_edges, lattice_state)
    populations_out = lattice_state.reshape(1, 19, slab_depth, lane_count)
    readings = [jnp.take(density.reshape(-1), probe_cell) for density in densities]
    gained = pressure_gain * (jnp.stack(readings, axis=1) - 1.0)
    previous = jnp.concatenate(
        [history[:, SAMPLES - 1 : SAMPLES].astype(jnp.float32), gained[:, :-1]], axis=1
    )
    rate_values = gained - previous
    recent = jnp.concatenate(
        [
            history[:, STEPS:SAMPLES],
            gained.astype(jnp.bfloat16),
            history[:, SAMPLES + STEPS :],
            rate_values.astype(jnp.bfloat16),
        ],
        axis=1,
    )
    transform = transform_table()
    count_slots = recent.shape[0]
    alive_slot = jnp.arange(count_slots, dtype=jnp.int32) < panel_count[0]
    outgoing = route_slots(recent, panel_owner, alive_slot, blocks)
    incoming = pl.pallas_call(
        functools.partial(exchange_kernel, blocks),
        out_shape=jax.ShapeDtypeStruct(outgoing.shape, outgoing.dtype),
        in_specs=[vmem],
        out_specs=vmem,
        scratch_shapes=[pltpu.VMEM(outgoing.shape, outgoing.dtype)]
        + [pltpu.SemaphoreType.DMA((blocks,))] * 2,
        compiler_params=pltpu.CompilerParams(collective_id=1, has_side_effects=True),
    )(outgoing)
    owned = settle(incoming).reshape(P_OWN, 2, SAMPLES)
    spectra = (
        jnp.einsum("pgt,tk->pgk", owned, transform, preferred_element_type=jnp.float32)
        .astype(jnp.bfloat16)
        .reshape(P_OWN, 4 * BINS)
    )
    panels = jnp.concatenate([spectra, panel_pos.T, panel_normal.T], axis=1)
    gathered = lax.all_gather(panels, "obs", axis=0, tiled=True).astype(jnp.float32)
    listeners = observers.shape[1]
    chunk = listeners // blocks
    spectrum = pl.pallas_call(
        functools.partial(radiate_kernel, blocks),
        out_shape=jax.ShapeDtypeStruct((chunk, 2 * BINS), jnp.float32),
        in_specs=[vmem, vmem],
        out_specs=vmem,
        scratch_shapes=[
            pltpu.VMEM(shape, jnp.float32)
            for shape in [
                (BINS, 8, listeners), (BINS, 8, listeners), (listeners, 2 * BINS),
                (blocks, chunk, 2 * BINS), (blocks, chunk, 2 * BINS),
            ]
        ]
        + [pltpu.SemaphoreType.DMA((blocks,))] * 2,
        compiler_params=pltpu.CompilerParams(collective_id=2, has_side_effects=True),
    )(gathered, observers)
    return (populations_out, spectrum[None])


def solution(mesh):
    placed = (
        P("blk", None, "obs", None),
        P("blk", None),
        P("blk", None),
        P(("blk", "obs")),
        P(("blk", "obs"), None),
        P(("blk", "obs")),
        P(("blk", "obs")),
        P(None, ("blk", "obs")),
        P(None, ("blk", "obs")),
        P(None, "obs"),
    )
    return jax.shard_map(
        body,
        mesh=mesh,
        in_specs=placed,
        out_specs=(P("blk", None, "obs", None), P("obs", "blk", None)),
        check_vma=False,
    )
```

time: 109 us -> 92.4 us (0.85)
  Pallas kernels: 87.7 us -> 72.7 us
  other arithmetic: 4.12 us -> 2.86 us
    pallas_call x1, Pallas kernels: 53.8 us -> 39.3 us  [body(): pl.pallas_call(functools.partial(window_kernel, blocks, ring), out_shape=...]
    concatenate x1 -> x0, other arithmetic: 1.26 us -> none  [body(): targets = jnp.concatenate([block_faces[0], block_edges[0]])]
where the time goes in v1:
time: 92.4 us; the launch traced here: 92.1 us
  Pallas kernels  72.7 us (79%)
  local copies, waits for them, and re-layouts  11.7 us (13%)
  other arithmetic  2.86 us (3%)
  blocking collectives  1.87 us (2%)
  between operations  1.64 us (2%)
  matrix products  1.35 us (1%)
    pallas_call x1, Pallas kernels, body(): pl.pallas_call(functools.partial(window_kernel, blocks, ring), out_shape=...  39.3 us
    pallas_call x1, Pallas kernels, body(): pl.pallas_call(functools.partial(radiate_kernel, blocks), out_shape=jax.S...  23.2 us
    pallas_call x1, Pallas kernels, body(): pl.pallas_call(functools.partial(exchange_kernel, blocks), out_shape=jax....  10.2 us
    gather x4, local copies, waits for them, and re-layouts, body(): jnp.take(density.reshape(-1), probe_cell)  4.59 us
    unnamed x25, local copies, waits for them, and re-layouts  3.07 us
    all_gather x1, blocking collectives, body(): lax.all_gather(panels, 'obs', axis=0, tiled=True).astype(jnp.float32)  1.87 us

profile of v1, /device:TPU:0, one launch (start us, length us, event | category | flops | bytes accessed | tf_op | source)
XLA Modules:
  0.0 92.1 jit_solution(6276965307424482002)
XLA Ops:
  0.6 39.3 %shard_map.113 = (f32[19,16,1024]{2,1,0:T(8,128)}, f32[4,16,1024]{2,1,0:T(8,128)}) custom-call(s32[1,4]{1,0:T(1,128)} %face_ref.1, s32[1,4]{1,0:T(1,128)} %rim_face_ref.1, f32[19,16,1024]{2,1,0:T(8,128)} %bitcast.56), custom_call_target="tpu_custom_call" | custom-call | tf_op jit(solution)/shard_map/pallas_call | solution.py:567
  39.9 1.0 %slice_bitcast_fusion.2 = (f32[2,8,8,128]{3,2,1,0:T(8,128)S(1)}, f32[2,8,8,128]{3,2,1,0:T(8,128)S(1)}, f32[2,8,8,128]{3,2,1,0:T(8,128)S(1)}, f32[2,8,8,128]{3,2,1,0:T(8,128)S(1)}) fusion(f32[4,16,1024]{2,1,0:T(8,128)} %get-tuple-element.6), kind=kLoop, calls=%fused_computation.38 | loop fusion | bytes 524288
  40.9 1.1 %gather_fusion.2 = f32[128]{0:T(128)S(1)} fusion(f32[16384]{0:T(1024)S(1)} %bitcast.51, s32[1024]{0:T(1024)S(1)} %pad_clamp_fusion.1), kind=kCustom, calls=%fused_computation.clone | custom fusion | bytes 1536 | tf_op jit(solution)/shard_map/jit(_take)/gather | solution.py:595
  42.1 1.1 %gather_fusion.3 = f32[128]{0:T(128)S(1)} fusion(f32[16384]{0:T(1024)S(1)} %bitcast.53, s32[1024]{0:T(1024)S(1)} %pad_clamp_fusion.1), kind=kCustom, calls=%fused_computation.1.clone | custom fusion | bytes 1536 | tf_op jit(solution)/shard_map/jit(_take)/gather | solution.py:595
  43.3 1.1 %gather_fusion.4 = f32[128]{0:T(128)S(1)} fusion(f32[16384]{0:T(1024)S(1)} %bitcast.54, s32[1024]{0:T(1024)S(1)} %pad_clamp_fusion.1), kind=kCustom, calls=%fused_computation.2.clone | custom fusion | bytes 1536 | tf_op jit(solution)/shard_map/jit(_take)/gather | solution.py:595
  44.5 1.1 %gather_fusion.5 = f32[128]{0:T(128)S(1)} fusion(f32[16384]{0:T(1024)S(1)} %bitcast.52, s32[1024]{0:T(1024)S(1)} %pad_clamp_fusion.1), kind=kCustom, calls=%fused_computation.3.clone | custom fusion | bytes 1536 | tf_op jit(solution)/shard_map/jit(_take)/gather | solution.py:595
  47.2 0.2 reduce_window_sum.11
  47.4 0.2 select_reduce_fusion.1
  47.7 0.8 gather_fusion
  48.8 1.2 %gather_fusion.1 = s32[128]{0:T(128)S(1)} fusion(s32[128]{0:T(128)S(1)} %copy-done, s32[1024]{0:T(1024)S(1)} %pad_clamp_fusion), kind=kCustom, calls=%fused_computation.5 | custom fusion | bytes 1536 | tf_op jit(solution)/shard_map/jit(_take)/gather | solution.py:531
  50.0 0.2 gather.38
  50.2 0.2 reduce_sum.29
  50.5 0.2 reduce_or.13
  50.8 0.7 pad_maximum_fusion.source_ref
  51.5 10.2 %shard_map.114 = bf16[16,8,513]{2,1,0:T(8,128)(2,1)} custom-call(bf16[16,8,513]{2,1,0:T(8,128)(2,1)} %pad_maximum_fusion.source_ref), custom_call_target="tpu_custom_call" | custom-call | tf_op jit(solution)/shard_map/pallas_call | solution.py:614
  61.7 0.8 slice.36
  62.6 1.2 %convolution_convert_fusion = bf16[64,512]{1,0:T(8,128)(2,1)S(1)} fusion(bf16[128,513]{1,0:T(8,128)(2,1)} %bitcast.58, s32[128]{0:T(128)S(1)} %bitcast_convert_fusion), kind=kOutput, calls=%fused_computation.6 | convolution fusion | flops 8429568 | bytes 197120 | tf_op jit(solution)/shard_map/rp,rw->pw/dot_general | solution.py:540
  63.8 0.3 cosine_convert_fusion
  64.1 0.2 fusion
  64.7 1.9 %all_gather.3 = bf16[128,262]{1,0:T(8,128)(2,1)S(1)} all-gather(bf16[64,262]{1,0:T(8,128)(2,1)S(1)} %pad_maximum_fusion.2), channel_id=1, replica_groups=mesh['blk'=16,'obs'=2] {'obs'}, dimensions={0}, use_global_device_ids=true | all-gather | bytes 100608 | tf_op jit(solution)/shard_map/all_gather | solution.py:630
  66.5 0.7 convert_element_type.49.panel_ref
  67.2 23.2 %shard_map.115 = f32[32,128]{1,0:T(8,128)} custom-call(f32[128,262]{1,0:T(8,128)} %convert_element_type.49.panel_ref, f32[3,512]{1,0:T(4,128)} %listen_ref.1), custom_call_target="tpu_custom_call" | custom-call | tf_op jit(solution)/shard_map/pallas_call | solution.py:633
  90.4 1.0 %copy.103 = f32[1,19,16,1024]{3,2,1,0:T(8,128)} copy(f32[1,19,16,1024]{3,2,1,0:T(8,128)S(1)} %bitcast.55) | data formatting | bytes 2490368
  91.5 0.6 copy.104
  (50 shorter events, 1.8 us)
Async XLA Ops:
  0.6 40.3 %copy-start.6 = (s32[128]{0:T(128)S(1)}, s32[128]{0:T(128)}, u32[]{:S(2)}) copy-start(s32[128]{0:T(128)} %param.15) | copy-start | bytes 1540
  40.9 4.8 %copy-start.2 = (bf16[128,512]{1,0:T(8,128)(2,1)S(1)}, bf16[128,512]{1,0:T(8,128)(2,1)}, u32[]{:S(2)}) copy-start(bf16[128,512]{1,0:T(8,128)(2,1)} %param.16) | copy-start | bytes 393220
  42.1 4.9 %copy-start = (s32[128]{0:T(128)S(1)}, s32[128]{0:T(128)}, u32[]{:S(2)}) copy-start(s32[128]{0:T(128)} %param.18) | copy-start | bytes 1540
  48.5 15.8 %copy-start.4 = (bf16[3,64]{1,0:T(4,128)(2,1)S(1)}, bf16[3,64]{1,0:T(4,128)(2,1)}, u32[]{:S(2)}) copy-start(bf16[3,64]{1,0:T(4,128)(2,1)} %param.19) | copy-start | bytes 1156
  48.5 15.9 %copy-start.5 = (bf16[3,64]{1,0:T(4,128)(2,1)S(1)}, bf16[3,64]{1,0:T(4,128)(2,1)}, u32[]{:S(2)}) copy-start(bf16[3,64]{1,0:T(4,128)(2,1)} %param.20) | copy-start | bytes 1156
  50.0 40.4 %copy-start.1 = (f32[19,16,1024]{2,1,0:T(8,128)S(1)}, f32[19,16,1024]{2,1,0:T(8,128)}, u32[]{:S(2)}) copy-start(f32[19,16,1024]{2,1,0:T(8,128)} %get-tuple-element.5) | copy-start | bytes 3735556
  90.4 1.1 %copy-start.3 = (f32[32,128]{1,0:T(8,128)S(1)}, f32[32,128]{1,0:T(8,128)}, u32[]{:S(2)}) copy-start(f32[32,128]{1,0:T(8,128)} %shard_map.115) | copy-start | bytes 49156

commit v2 on v1

v2 whole, which is shorter than its diff:
```python
import functools
import math

import jax
import jax.numpy as jnp
import numpy as np
from jax import lax
from jax.experimental import pallas as pl
from jax.experimental.pallas import tpu as pltpu
from jax.sharding import PartitionSpec as P

BS = 32
STEPS = 4
SAMPLES = 256
BINS = 64
P_OWN = 64


velocity_list = [
    (0, 0, 0),
    (1, 0, 0),
    (-1, 0, 0),
    (0, 1, 0),
    (0, -1, 0),
    (0, 0, 1),
    (0, 0, -1),
    (1, 1, 0),
    (-1, -1, 0),
    (1, -1, 0),
    (-1, 1, 0),
    (1, 0, 1),
    (-1, 0, -1),
    (1, 0, -1),
    (-1, 0, 1),
    (0, 1, 1),
    (0, -1, -1),
    (0, 1, -1),
    (0, -1, 1),
]
weight_list = [1.0 / 3.0] + [1.0 / 18.0] * 6 + [1.0 / 36.0] * 12
x_moving = [1, 2, 7, 8, 9, 10, 11, 12, 13, 14]
y_upward = [3, 7, 10, 15, 17]
y_downward = [4, 8, 9, 16, 18]
z_upward = [5, 11, 14, 15, 18]
z_downward = [6, 12, 13, 16, 17]
relax_rate = 1.6
pressure_gain = 60.0
sound_speed = 0.5


x_plus = [1, 7, 9, 11, 13]
x_minus = [2, 8, 10, 12, 14]
x_order = x_plus + x_minus
still = [0, 3, 4, 5, 6, 15, 16, 17, 18]
LANES = 128
FACE = 256


def collide_tile(f):
    sums = [None] * 19
    gaps = [None] * 19
    for number in range(1, 19, 2):
        sums[number] = f[number] + f[number + 1]
        gaps[number] = f[number] - f[number + 1]
    density = f[0]
    for number in range(1, 19, 2):
        density = density + sums[number]
    speeds = []
    for axis in range(3):
        total = None
        for number in range(1, 19, 2):
            sign = velocity_list[number][axis]
            if sign == 0:
                continue
            if total is None:
                total = gaps[number]
            elif sign == 1:
                total = total + gaps[number]
            else:
                total = total - gaps[number]
        speeds.append(total)
    inverse = 1.0 / density
    speeds = [speed * inverse for speed in speeds]
    squared = speeds[0] * speeds[0] + speeds[1] * speeds[1] + speeds[2] * speeds[2]
    base = 1.0 - 1.5 * squared
    keep = 1.0 - relax_rate
    out = [None] * 19
    out[0] = keep * f[0] + ((relax_rate * weight_list[0]) * density) * base
    scaled = {}
    thrice = {}
    for weight in sorted(set(weight_list[1:])):
        scaled[weight] = (relax_rate * weight) * density
        thrice[weight] = 3.0 * scaled[weight]
    for number in range(1, 19, 2):
        projected = None
        for axis in range(3):
            sign = velocity_list[number][axis]
            if sign == 0:
                continue
            if projected is None:
                projected = speeds[axis]
            elif sign == 1:
                projected = projected + speeds[axis]
            else:
                projected = projected - speeds[axis]
        weight = weight_list[number]
        even = scaled[weight] * (base + 4.5 * (projected * projected))
        odd = thrice[weight] * projected
        out[number] = keep * f[number] + (even + odd)
        out[number + 1] = keep * f[number + 1] + (even - odd)
    return out


def lane_of(shape):
    return lax.broadcasted_iota(jnp.int32, shape, 1)


def turned(value, amount):
    amount = amount % value.shape[1]
    return value if amount == 0 else pltpu.roll(value, amount, 1)


def pushed(value, low, high, sign):
    if sign == 1:
        return jnp.concatenate([low, value[:-1]], axis=0)
    return jnp.concatenate([value[1:], high], axis=0)


def shift_of(number):
    return velocity_list[number][1] * BS + velocity_list[number][2]


face_sets = [y_downward, y_upward, z_downward, z_upward]


def pack_tile(values, tile, tiles, chosen_numbers, columns, rows):
    depth = values[chosen_numbers[0]].shape[0]
    spot = lane_of((depth, LANES)) % BS
    quarter = lane_of((depth, LANES)) // BS
    u = tile % 4
    for side, (chosen, begin) in enumerate([(z_downward, 0), (z_upward, BS - 1)]):
        for j, number in enumerate(chosen):
            if number in chosen_numbers:
                moved = turned(values[number] - weight_list[number], 8 * u + j - begin)
                columns[side] = jnp.where(spot == 8 * u + j, moved, columns[side])
    for side, (chosen, at, begin) in enumerate(
        [(y_downward, 0, 0), (y_upward, tiles - 1, LANES - BS)]
    ):
        if tile != at:
            continue
        for j, number in enumerate(chosen):
            if number in chosen_numbers:
                moved = turned(values[number] - weight_list[number], j % 4 * BS - begin)
                rows[side][j // 4] = jnp.where(quarter == j % 4, moved, rows[side][j // 4])


def collide_all(field_ref, rolled_ref, moving_ref, edge_ref, draft_ref):
    depth = field_ref.shape[1]
    tiles = field_ref.shape[2] // LANES
    blank = jnp.zeros((depth, LANES), jnp.float32)
    rows = [[blank, blank], [blank, blank]]
    for half in range(tiles // 4):
        columns = [blank, blank]
        for u in range(4):
            tile = half * 4 + u
            lanes = slice(tile * LANES, (tile + 1) * LANES)
            out = collide_tile([field_ref[number, :, lanes] for number in range(19)])
            for number in range(19):
                if number in still:
                    rolled_ref[tile + 1, number] = turned(out[number], shift_of(number))
                else:
                    moving_ref[tile, x_order.index(number)] = out[number]
            for place, number in enumerate(x_plus):
                edge_ref[0, place, tile : tile + 1, :] = out[number][depth - 1 : depth]
            for place, number in enumerate(x_minus):
                edge_ref[1, place, tile : tile + 1, :] = out[number][0:1]
            pack_tile(out, tile, tiles, still, columns, rows)
        for side in range(2):
            draft_ref[2 + side, :, half * LANES : (half + 1) * LANES] = columns[side]
    for side in range(2):
        for half in range(2):
            draft_ref[side, :, half * LANES : (half + 1) * LANES] = rows[side][half]


def shifted(moving_ref, near_ref, tile, number):
    place = x_order.index(number)
    low = near_ref[0, place % 5, tile : tile + 1, :]
    high = near_ref[1, place % 5, tile : tile + 1, :]
    return pushed(moving_ref[tile, place], low, high, velocity_list[number][0])


def pack_moving(moving_ref, near_ref, draft_ref, piece_ref):
    tiles = moving_ref.shape[0]
    crossing = x_order[1:5] + x_order[6:]

    def draft(piece, half):
        return draft_ref[piece, :, half * LANES : (half + 1) * LANES]

    rows = [[draft(side, half) for half in range(2)] for side in range(2)]
    for half in range(tiles // 4):
        columns = [draft(2 + side, half) for side in range(2)]
        for u in range(4):
            tile = half * 4 + u
            values = {}
            for number in crossing:
                if velocity_list[number][1] == 0 or tile in (0, tiles - 1):
                    values[number] = shifted(moving_ref, near_ref, tile, number)
            pack_tile(values, tile, tiles, list(values), columns, rows)
        for side in range(2):
            piece_ref[2 + side, :, half * LANES : (half + 1) * LANES] = columns[side].astype(jnp.bfloat16)
    for side in range(2):
        for half in range(2):
            piece_ref[side, :, half * LANES : (half + 1) * LANES] = rows[side][half].astype(jnp.bfloat16)


def roll_moving(rolled_ref, moving_ref, near_ref):
    tiles = moving_ref.shape[0]
    for tile in range(tiles):
        for number in x_order:
            value = shifted(moving_ref, near_ref, tile, number)
            rolled_ref[tile + 1, number] = turned(value, shift_of(number))


def finish_step(face, edge, got_ref, rolled_ref, field_ref, density_ref):
    depth = field_ref.shape[1]
    tiles = field_ref.shape[2] // LANES
    lane = lane_of((depth, LANES))
    spot = lane % BS

    def arrived(source, half):
        return got_ref[source, :, half * LANES : (half + 1) * LANES].astype(jnp.float32)

    corners = {15: (0, 0, 1), 17: (1, 1, 31), 18: (2, 1, 65), 16: (3, 0, 31)}
    corner_lane = {15: 0, 17: BS - 1, 18: LANES - BS, 16: LANES - 1}
    for piece, source, pad, begin in [(1, face[0], 0, 0), (0, face[1], tiles + 1, LANES - BS)]:
        halves = [arrived(source, half) for half in range(2)]
        for j, number in enumerate(face_sets[piece]):
            shift_z = velocity_list[number][2]
            value = turned(halves[j // 4], begin + shift_z - j % 4 * BS)
            if number in corners:
                which, half, amount = corners[number]
                corner = turned(arrived(edge[which], half), amount)
                value = jnp.where(lane == corner_lane[number], corner, value)
            rolled_ref[pad, number] = value + weight_list[number]
    columns = {}
    for piece, source, rim in [(3, face[2], 0), (2, face[3], BS - 1)]:
        chosen = face_sets[piece]
        halves = [arrived(source, half) for half in range(2)]
        for tile in range(tiles):
            for j, number in enumerate(chosen):
                shift_y = velocity_list[number][1]
                amount = rim - 8 * (tile % 4) - j + BS * shift_y
                column = turned(halves[tile // 4], amount) + weight_list[number]
                value = jnp.where(spot == rim, column, rolled_ref[tile + 1, number])
                if shift_y != 0:
                    rolled_ref[tile + 1, number] = value
                else:
                    columns[tile, number] = value
                    field_ref[number, :, tile * LANES : (tile + 1) * LANES] = value
    for tile in range(tiles):
        lanes = slice(tile * LANES, (tile + 1) * LANES)
        total = None
        for number, (_, shift_y, shift_z) in enumerate(velocity_list):
            if shift_y == 0 and shift_z != 0:
                value = field_ref[number, :, lanes]
            else:
                value = rolled_ref[tile + 1, number]
                if shift_y == 1:
                    value = jnp.where(lane < BS, rolled_ref[tile, number], value)
                elif shift_y == -1:
                    value = jnp.where(lane >= LANES - BS, rolled_ref[tile + 2, number], value)
                field_ref[number, :, lanes] = value
            total = value if total is None else total + value
        density_ref[:, lanes] = total


def joined(left, right, left_axis, right_axis):
    return lax.dot_general(
        left.astype(jnp.bfloat16), right.astype(jnp.bfloat16),
        (((left_axis,), (right_axis,)), ((), ())), preferred_element_type=jnp.float32,
    )


def rows_of(shape):
    return lax.broadcasted_iota(jnp.int32, shape, 0)


def route(blocks, owner_ref, count, history_ref, select_ref, send_ref):
    slots = owner_ref.shape[1]
    room = send_ref.shape[1]
    width = history_ref.shape[1]
    owner = owner_ref[...]
    alive = lane_of((1, slots)) < count
    target = lax.shift_right_logical(owner, P_OWN.bit_length() - 1)
    spot = lax.bitwise_and(owner, P_OWN - 1)
    member = jnp.where((rows_of((blocks, slots)) == target) & alive, 1.0, 0.0)
    earlier = jnp.where(rows_of((slots, slots)) < lane_of((slots, slots)), 1.0, 0.0)
    before = joined(member, earlier, 1, 0)
    order = jnp.sum(before * member, axis=0, keepdims=True).astype(jnp.int32)
    label = jnp.where(alive, target * room + order, -1)
    select = jnp.where(rows_of((blocks * room, slots)) == label, 1.0, 0.0)
    select_ref[...] = select.astype(jnp.bfloat16)
    moved = joined(select, history_ref[...], 1, 0)
    spots = joined(select, jnp.where(rows_of((P_OWN, slots)) == spot, 1.0, 0.0), 1, 1)
    for block in range(blocks):
        rows = slice(block * room, (block + 1) * room)
        send_ref[block, :, 0:width] = moved[rows].astype(jnp.bfloat16)
        send_ref[block, :, width : width + P_OWN] = spots[rows].astype(jnp.bfloat16)


def unpacked(got_ref, flat_ref):
    blocks, room = got_ref.shape[0], got_ref.shape[1]
    for block in range(blocks):
        flat_ref[block * room : (block + 1) * room, :] = got_ref[block].astype(jnp.float32)


def settle_history(got_ref, flat_ref, choose_ref, table_ref, partial_ref):
    unpacked(got_ref, flat_ref)
    choose = flat_ref[:, 2 * SAMPLES : 2 * SAMPLES + P_OWN].astype(jnp.bfloat16)
    choose_ref[...] = choose
    owned = joined(choose, flat_ref[:, 0 : 2 * SAMPLES], 0, 0)
    for field in range(2):
        partial_ref[:, field * 2 * BINS : (field + 1) * 2 * BINS] = joined(
            owned[:, field * SAMPLES : (field + 1) * SAMPLES], table_ref[...], 1, 0
        )


def reading_of(density_ref, cell_ref, probe_ref):
    depth = density_ref.shape[0]
    count = density_ref.shape[1]
    excess = density_ref[...] - 1.0
    parts = []
    for _ in range(3):
        part = excess.astype(jnp.bfloat16).astype(jnp.float32)
        parts.append(part)
        excess = excess - part
    found = joined(jnp.concatenate(parts, axis=0), cell_ref[...], 1, 0)
    layers = found[0:depth] + found[depth : 2 * depth] + found[2 * depth : 3 * depth]
    layer = lax.div(probe_ref[...], count)
    mine = rows_of(layers.shape) == layer
    return jnp.sum(jnp.where(mine, layers, 0.0), axis=0, keepdims=True)


def window_kernel(
    blocks, ring, face_ref, rim_face_ref, count_ref, start_ref, owner_ref, probe_ref, history_ref,
    place_ref, normal_ref, table_ref, tail_ref, field_ref, spectra_ref, place_out_ref,
    density_ref, rolled_ref, moving_ref, edge_ref, near_ref, draft_ref, piece_ref,
    send_ref, got_even, got_odd, select_ref, cell_ref, past_send, past_got, flat_ref, choose_ref,
    partial_ref, fresh_ref, fresh_send, fresh_got, fresh_flat, done_ref, done_got, spot_ref, spot_got,
    edge_send, edge_got, send_sem, got_sem, past_send_sem, past_got_sem, fresh_send_sem, fresh_got_sem,
    done_send_sem, done_got_sem, spot_send_sem, spot_got_sem,
):
    mesh_ids = pl.DeviceIdType.MESH
    me = lax.axis_index("blk")
    side = lax.axis_index("obs")
    right = lax.rem(side + 1, ring)
    left = lax.rem(side + ring - 1, ring)
    barrier = pltpu.get_barrier_semaphore()
    slots = owner_ref.shape[1]

    def greet(distance, carry):
        peer = lax.rem(me + distance, blocks)
        pl.semaphore_signal(barrier, inc=1, device_id=(peer, side), device_id_type=mesh_ids)
        return carry

    for distance in range(1, ring):
        beside = lax.rem(side + distance, ring)
        pl.semaphore_signal(barrier, inc=1, device_id=(me, beside), device_id_type=mesh_ids)
    lax.fori_loop(1, blocks, greet, 0)
    face = [face_ref[0, k] for k in range(4)]
    edge = [rim_face_ref[0, k] for k in range(4)]
    field_ref[...] = start_ref[...]
    route(blocks, owner_ref, count_ref[0], history_ref, select_ref, past_send)
    cell = lax.rem(probe_ref[...], start_ref.shape[2])
    cell_ref[...] = jnp.where(rows_of(cell_ref.shape) == cell, 1.0, 0.0).astype(jnp.bfloat16)
    spot_ref[...] = jnp.zeros_like(spot_ref)
    spot_ref[0:3, 0:P_OWN] = place_ref[...].astype(jnp.float32)
    spot_ref[3:6, 0:P_OWN] = normal_ref[...].astype(jnp.float32)
    fresh_ref[...] = jnp.zeros_like(fresh_ref)

    def swap(source_of, into_ref, send_sems, got_sems, distance):
        peer = lax.rem(me + distance, blocks)
        return pltpu.make_async_remote_copy(
            src_ref=source_of(distance, peer),
            dst_ref=into_ref.at[me],
            send_sem=send_sems.at[distance],
            recv_sem=got_sems.at[distance],
            device_id=(peer, side),
            device_id_type=mesh_ids,
        )

    def every(action):
        def visit(distance, inner):
            action(distance)
            return inner

        lax.fori_loop(1, blocks, visit, 0)

    def past_copy(distance):
        return swap(lambda _, peer: past_send.at[peer], past_got, past_send_sem, past_got_sem, distance)

    def fresh_copy(distance):
        return swap(lambda _, peer: fresh_send.at[peer], fresh_got, fresh_send_sem, fresh_got_sem, distance)

    def ring_copies(source_ref, into_ref, send_sems, got_sems):
        return [
            pltpu.make_async_remote_copy(
                src_ref=source_ref,
                dst_ref=into_ref.at[side],
                send_sem=send_sems.at[distance],
                recv_sem=got_sems.at[distance],
                device_id=(me, lax.rem(side + distance, ring)),
                device_id_type=mesh_ids,
            )
            for distance in range(1, ring)
        ]

    def note(step):
        gained = pressure_gain * reading_of(density_ref.at[step], cell_ref, probe_ref)
        if step == 0:
            last = jnp.where(lane_of((8, 2 * SAMPLES)) == SAMPLES - 1, 1.0, 0.0)
            before = joined(last, history_ref[...], 1, 1)[0:1]
        else:
            before = fresh_ref[step - 1 : step, :]
        fresh_ref[step : step + 1, :] = gained
        fresh_ref[STEPS + step : STEPS + step + 1, :] = gained - before

    def one_step(step):
        got_ref = got_odd if step % 2 else got_even
        collide_all(field_ref, rolled_ref, moving_ref, edge_ref, draft_ref)
        if step == 0:
            pl.semaphore_wait(barrier, blocks + ring - 2)
        edges = [
            pltpu.make_async_remote_copy(
                src_ref=edge_ref.at[way],
                dst_ref=near_ref.at[step, way],
                send_sem=edge_send.at[step, way],
                recv_sem=edge_got.at[step, way],
                device_id=(me, beside),
                device_id_type=mesh_ids,
            )
            for way, beside in enumerate([right, left])
        ]
        for copy in edges:
            copy.start()
        for copy in edges:
            copy.wait()
        pack_moving(moving_ref, near_ref.at[step], draft_ref, piece_ref)

        def copy_to(distance):
            return swap(
                lambda number, _: send_ref.at[number], got_ref, send_sem.at[step], got_sem.at[step], distance
            )

        def begin(distance):
            peer = lax.rem(me + distance, blocks)
            up = (peer == face[1]) | (peer == edge[2]) | (peer == edge[3])
            piece = jnp.where(peer == face[3], 3, jnp.where(peer == face[2], 2, up.astype(jnp.int32)))
            send_ref[distance] = piece_ref[piece]
            copy_to(distance).start()

        every(begin)
        roll_moving(rolled_ref, moving_ref, near_ref.at[step])
        if step == 0:
            every(lambda distance: past_copy(distance).start())
            for copy in ring_copies(spot_ref, spot_got, spot_send_sem, spot_got_sem):
                copy.start()
            past_got[me] = past_send[me]
        else:
            note(step - 1)
        if step == 2:
            every(lambda distance: past_copy(distance).wait())
            settle_history(past_got, flat_ref, choose_ref, table_ref, partial_ref)
        every(lambda distance: copy_to(distance).wait())
        finish_step(face, edge, got_ref, rolled_ref, field_ref, density_ref.at[step])

    for step in range(STEPS):
        one_step(step)
    note(STEPS - 1)
    fresh = joined(select_ref[...], fresh_ref[...], 1, 1)
    room = fresh_send.shape[1]
    for block in range(blocks):
        fresh_send[block] = fresh[block * room : (block + 1) * room].astype(jnp.bfloat16)
    every(lambda distance: fresh_copy(distance).start())
    fresh_got[me] = fresh_send[me]
    for copy in ring_copies(spot_ref, spot_got, spot_send_sem, spot_got_sem):
        copy.wait()
    spot_got[side] = spot_ref[...]
    place_out_ref[...] = spot_got[...]
    every(lambda distance: fresh_copy(distance).wait())
    unpacked(fresh_got, fresh_flat)
    newest = joined(choose_ref[...], fresh_flat[...], 0, 0)
    total = partial_ref[...] + joined(newest, tail_ref[...], 1, 0)
    done_ref[...] = total.astype(jnp.bfloat16)
    copies = ring_copies(done_ref, done_got, done_send_sem, done_got_sem)
    for copy in copies:
        copy.start()
    done_got[side] = done_ref[...]
    for copy in copies:
        copy.wait()
    spectra_ref[...] = done_got[...].astype(jnp.float32)


def transform_tables():
    moments = np.arange(SAMPLES)[:, None]
    harmonics = np.arange(BINS)[None, :] + 1
    turns = moments * harmonics % SAMPLES
    phases = turns.astype(np.float32) * np.float32(2.0 * math.pi / SAMPLES)
    table = np.concatenate([np.cos(phases), -np.sin(phases)], axis=1).astype(jnp.bfloat16)
    past = np.zeros_like(table)
    past[STEPS:] = table[: SAMPLES - STEPS]
    tail = np.zeros((LANES, 4 * BINS), table.dtype)
    for field in range(2):
        rows = slice(field * STEPS, (field + 1) * STEPS)
        tail[rows, field * 2 * BINS : (field + 1) * 2 * BINS] = table[SAMPLES - STEPS :]
    return jnp.asarray(past), jnp.asarray(tail)


def greet_peers(blocks):
    me = lax.axis_index("blk")
    side = lax.axis_index("obs")
    barrier = pltpu.get_barrier_semaphore()

    def greet(distance, carry):
        pl.semaphore_signal(
            barrier, inc=1, device_id=(lax.rem(me + distance, blocks), side),
            device_id_type=pl.DeviceIdType.MESH,
        )
        return carry

    lax.fori_loop(1, blocks, greet, 0)
    return barrier


def swap_pieces(blocks, send_ref, got_ref, send_sem, got_sem):
    me = lax.axis_index("blk")
    side = lax.axis_index("obs")

    def copy_to(distance):
        peer = lax.rem(me + distance, blocks)
        return pltpu.make_async_remote_copy(
            src_ref=send_ref.at[peer],
            dst_ref=got_ref.at[me],
            send_sem=send_sem.at[distance],
            recv_sem=got_sem.at[distance],
            device_id=(peer, side),
            device_id_type=pl.DeviceIdType.MESH,
        )

    def begin(distance, inner):
        copy_to(distance).start()
        return inner

    def finish(distance, inner):
        copy_to(distance).wait()
        return inner

    lax.fori_loop(1, blocks, begin, 0)
    lax.fori_loop(1, blocks, finish, 0)


def radiate_kernel(
    blocks, panel_ref, listen_ref, out_ref,
    real_ref, imag_ref, full_ref, send_ref, got_ref, send_sem, got_sem,
):
    barrier = greet_peers(blocks)
    listeners = listen_ref.shape[1]
    real_ref[...] = jnp.zeros_like(real_ref)
    imag_ref[...] = jnp.zeros_like(imag_ref)
    step_angle = 2.0 * math.pi / SAMPLES / sound_speed

    def accumulate(block_number, carry):
        begin = pl.multiple_of(block_number * 8, 8)
        panel = panel_ref[pl.ds(begin, 8), :]
        distance_sq = None
        facing = None
        for axis in range(3):
            at = 4 * BINS + axis
            offset = listen_ref[axis : axis + 1, :] - panel[:, at : at + 1]
            square = offset * offset
            along = panel[:, at + 3 : at + 4] * offset
            distance_sq = square if distance_sq is None else distance_sq + square
            facing = along if facing is None else facing + along
        distance = jnp.sqrt(distance_sq)
        far_term = facing / (4.0 * math.pi * sound_speed * distance_sq)
        ratio = sound_speed / distance
        angle = step_angle * distance
        turn_cos = jnp.cos(angle)
        turn_sin = jnp.sin(angle)
        wave_cos = far_term * turn_cos
        wave_sin = far_term * turn_sin
        for k in range(BINS):
            press_real = panel[:, k : k + 1]
            press_imag = panel[:, BINS + k : BINS + k + 1]
            rate_real = panel[:, 2 * BINS + k : 2 * BINS + k + 1]
            rate_imag = panel[:, 3 * BINS + k : 3 * BINS + k + 1]
            mixed_real = rate_real + ratio * press_real
            mixed_imag = rate_imag + ratio * press_imag
            real_ref[k] += mixed_real * wave_cos + mixed_imag * wave_sin
            imag_ref[k] += mixed_imag * wave_cos - mixed_real * wave_sin
            if k + 1 < BINS:
                wave_cos, wave_sin = (
                    wave_cos * turn_cos - wave_sin * turn_sin,
                    wave_sin * turn_cos + wave_cos * turn_sin,
                )
        return carry

    lax.fori_loop(0, panel_ref.shape[0] // 8, accumulate, 0)
    both = jnp.concatenate([jnp.sum(real_ref[...], axis=1), jnp.sum(imag_ref[...], axis=1)], axis=0)
    full_ref[...] = both.T
    chunk = out_ref.shape[0]
    for number in range(blocks):
        send_ref[number] = full_ref[number * chunk : (number + 1) * chunk]
    me = lax.axis_index("blk")
    got_ref[me] = send_ref[me]
    pl.semaphore_wait(barrier, blocks - 1)
    swap_pieces(blocks, send_ref, got_ref, send_sem, got_sem)
    out_ref[...] = jnp.sum(got_ref[...], axis=0)


def body(
    populations,
    block_faces,
    block_edges,
    probe_cell,
    history,
    panel_count,
    panel_owner,
    panel_pos,
    panel_normal,
    observers,
):
    blocks = lax.axis_size("blk")
    lattice_state = populations[0]
    slab_depth = lattice_state.shape[1]
    lane_count = lattice_state.shape[2]
    ring = lax.axis_size("obs")
    tiles = lane_count // LANES
    vmem = pl.BlockSpec(memory_space=pltpu.VMEM)
    smem = pl.BlockSpec(memory_space=pltpu.SMEM)
    wide = jnp.float32
    half = jnp.bfloat16
    slots = panel_owner.shape[0]
    room = -(-slots // blocks)
    past, tail = transform_tables()
    dma = pltpu.SemaphoreType.DMA
    lattice_state, spectra, places = pl.pallas_call(
        functools.partial(window_kernel, blocks, ring),
        out_shape=[
            jax.ShapeDtypeStruct((19, slab_depth, lane_count), wide),
            jax.ShapeDtypeStruct((ring, P_OWN, 4 * BINS), wide),
            jax.ShapeDtypeStruct((ring, 8, LANES), wide),
        ],
        in_specs=[smem] * 3 + [vmem] * 8,
        out_specs=[vmem] * 3,
        scratch_shapes=[
            pltpu.VMEM((STEPS, slab_depth, lane_count), wide),
            pltpu.VMEM((tiles + 2, 19, slab_depth, LANES), wide),
            pltpu.VMEM((tiles, len(x_order), slab_depth, LANES), wide),
            pltpu.VMEM((2, 5, tiles, LANES), wide),
            pltpu.VMEM((STEPS, 2, 5, tiles, LANES), wide),
            pltpu.VMEM((4, slab_depth, FACE), wide),
            pltpu.VMEM((4, slab_depth, FACE), half),
            pltpu.VMEM((blocks, slab_depth, FACE), half),
            pltpu.VMEM((blocks, slab_depth, FACE), half),
            pltpu.VMEM((blocks, slab_depth, FACE), half),
            pltpu.VMEM((blocks * room, slots), half),
            pltpu.VMEM((lane_count, slots), half),
            pltpu.VMEM((blocks, room, 5 * LANES), half),
            pltpu.VMEM((blocks, room, 5 * LANES), half),
            pltpu.VMEM((blocks * room, 5 * LANES), wide),
            pltpu.VMEM((blocks * room, P_OWN), half),
            pltpu.VMEM((P_OWN, 4 * BINS), wide),
            pltpu.VMEM((LANES, slots), wide),
            pltpu.VMEM((blocks, room, LANES), half),
            pltpu.VMEM((blocks, room, LANES), half),
            pltpu.VMEM((blocks * room, LANES), wide),
            pltpu.VMEM((P_OWN, 4 * BINS), half),
            pltpu.VMEM((ring, P_OWN, 4 * BINS), half),
            pltpu.VMEM((8, LANES), wide),
            pltpu.VMEM((ring, 8, LANES), wide),
        ]
        + [dma((STEPS, 2))] * 2
        + [dma((STEPS, blocks))] * 2
        + [dma((blocks,))] * 4
        + [dma((ring,))] * 4,
        compiler_params=pltpu.CompilerParams(collective_id=0, has_side_effects=True),
    )(
        block_faces, block_edges, panel_count, lattice_state, panel_owner[None], probe_cell[None],
        history, panel_pos, panel_normal, past, tail,
    )
    populations_out = lattice_state.reshape(1, 19, slab_depth, lane_count)
    places = places[:, :, :P_OWN].transpose(0, 2, 1).reshape(ring * P_OWN, 8)
    gathered = jnp.concatenate([spectra.reshape(ring * P_OWN, 4 * BINS), places], axis=1)
    listeners = observers.shape[1]
    chunk = listeners // blocks
    spectrum = pl.pallas_call(
        functools.partial(radiate_kernel, blocks),
        out_shape=jax.ShapeDtypeStruct((chunk, 2 * BINS), jnp.float32),
        in_specs=[vmem, vmem],
        out_specs=vmem,
        scratch_shapes=[
            pltpu.VMEM(shape, jnp.float32)
            for shape in [
                (BINS, 8, listeners), (BINS, 8, listeners), (listeners, 2 * BINS),
                (blocks, chunk, 2 * BINS), (blocks, chunk, 2 * BINS),
            ]
        ]
        + [pltpu.SemaphoreType.DMA((blocks,))] * 2,
        compiler_params=pltpu.CompilerParams(collective_id=2, has_side_effects=True),
    )(gathered, observers)
    return (populations_out, spectrum[None])


def solution(mesh):
    placed = (
        P("blk", None, "obs", None),
        P("blk", None),
        P("blk", None),
        P(("blk", "obs")),
        P(("blk", "obs"), None),
        P(("blk", "obs")),
        P(("blk", "obs")),
        P(None, ("blk", "obs")),
        P(None, ("blk", "obs")),
        P(None, "obs"),
    )
    return jax.shard_map(
        body,
        mesh=mesh,
        in_specs=placed,
        out_specs=(P("blk", None, "obs", None), P("obs", "blk", None)),
        check_vma=False,
    )
```

time: 92.4 us -> 78.1 us (0.85)
  local copies, waits for them, and re-layouts: 11.7 us -> 3.87 us
  blocking collectives: 1.87 us -> 0 us
  Pallas kernels: 72.7 us -> 71.1 us
  matrix products: 1.35 us -> 0 us
  other arithmetic: 2.86 us -> 1.6 us
    pallas_call x1 -> x0, Pallas kernels: 10.2 us -> none  [body(): pl.pallas_call(functools.partial(exchange_kernel, blocks), out_shape=jax....]
    pallas_call x1, Pallas kernels: 39.3 us -> 47.8 us  [body(): pl.pallas_call(functools.partial(window_kernel, blocks, ring), out_shape=...]
    gather x7 -> x0, local copies, waits for them, and re-layouts: 6.87 us -> none  [the longest x4 4.59 us: body(): jnp.take(density.reshape(-1), probe_cell)]
    all_gather x1 -> x0, blocking collectives: 1.87 us -> none  [body(): lax.all_gather(panels, 'obs', axis=0, tiled=True).astype(jnp.float32)]
    dot_general x2 -> x0, matrix products: 1.35 us -> none  [the longest x1 1.2 us: settle(): jnp.einsum('rp,rw->pw', choose, flat[:, :width], preferred_element_type=j...]
    slice x3 -> x0, local copies, waits for them, and re-layouts: 0.96 us -> none  [the longest x1 0.76 us: settle(): spots = flat[:, width].astype(jnp.int32)]
    unnamed x25 -> x4, local copies, waits for them, and re-layouts: 3.07 us -> 3.08 us
where the time goes in v2:
time: 78.1 us; the launch traced here: 77.9 us
  Pallas kernels  71.1 us (91%)
  local copies, waits for them, and re-layouts  3.87 us (5%)
  other arithmetic  1.6 us (2%)
  between operations  1.31 us (2%)
    pallas_call x1, Pallas kernels, body(): pl.pallas_call(functools.partial(window_kernel, blocks, ring), out_shape=...  47.8 us
    pallas_call x1, Pallas kernels, body(): pl.pallas_call(functools.partial(radiate_kernel, blocks), out_shape=jax.S...  23.3 us
    unnamed x4, local copies, waits for them, and re-layouts  3.08 us
    concatenate x1, other arithmetic, body(): jnp.concatenate([spectra.reshape(ring * P_OWN, 4 * BINS), places], axis=1)  1.6 us

profile of v2, /device:TPU:0, one launch (start us, length us, event | category | flops | bytes accessed | tf_op | source)
XLA Modules:
  0.0 77.9 jit_solution(13927969706021411826)
XLA Ops:
  1.3 47.8 %shard_map.131 = (f32[19,16,1024]{2,1,0:T(8,128)}, f32[2,64,256]{2,1,0:T(8,128)}, f32[2,8,128]{2,1,0:T(8,128)}) custom-call(s32[1,4]{1,0:T(1,128)} %face_ref.1, s32[1,4]{1,0:T(1,128)} %rim_face_ref.1, s32[1]{0:T(128)S(6)} %copy.17.count_ref, f32[19,16,1024]{2,1,0:T(8,128)} %bitcast.10, s32[1,128]{1,0:T(1,128)} %bitcast.14, s32[1,128]{1,0:T(1,128)} %bitcast.15, ...), custom_call_target="tpu_custom_call" | custom-call | tf_op jit(solution)/shard_map/pallas_call | solution.py:647
  49.1 0.7 slice_bitcast_fusion
  49.8 0.1 copy.14
  49.9 1.6 %pad_maximum_fusion.panel_ref = f32[128,264]{1,0:T(8,128)} fusion(f32[128,8]{1,0:T(8,128)S(1)} %bitcast.11, f32[128,256]{1,0:T(8,128)} %bitcast.12), kind=kLoop, calls=%fused_computation | loop fusion | flops 33792 | bytes 270336 | tf_op jit(solution)/shard_map/concatenate | solution.py:694
  51.5 23.3 %shard_map.132 = f32[32,128]{1,0:T(8,128)} custom-call(f32[128,264]{1,0:T(8,128)} %pad_maximum_fusion.panel_ref, f32[3,512]{1,0:T(4,128)} %listen_ref.1), custom_call_target="tpu_custom_call" | custom-call | tf_op jit(solution)/shard_map/pallas_call | solution.py:697
  74.8 0.0 copy-start
  74.8 2.5 %copy.18 = f32[1,19,16,1024]{3,2,1,0:T(8,128)} copy(f32[1,19,16,1024]{3,2,1,0:T(8,128)} %bitcast.9) | data formatting | bytes 2490368
  77.3 0.0 copy-done
  77.3 0.6 copy.19
Async XLA Ops:
  74.8 2.5 %copy-start = (f32[32,128]{1,0:T(8,128)S(1)}, f32[32,128]{1,0:T(8,128)}, u32[]{:S(2)}) copy-start(f32[32,128]{1,0:T(8,128)} %shard_map.132) | copy-start | bytes 49156

commit v3 on v2

--- a/solution.py
+++ b/solution.py
@@ -341,14 +341,117 @@
     return jnp.sum(jnp.where(mine, layers, 0.0), axis=0, keepdims=True)
 
 
+def prepare_waves(spot_got, listen_ref, wave_ref):
+    ring = spot_got.shape[0]
+    tiles = wave_ref.shape[0]
+    angle_step = 2.0 * math.pi / SAMPLES / sound_speed
+    for owner in range(ring):
+        columns = spot_got[owner].T
+
+        def one_group(group, columns=columns):
+            rows = slice(group * 8, (group + 1) * 8)
+            for tile in range(tiles):
+                lanes = slice(tile * LANES, (tile + 1) * LANES)
+                distance_sq = None
+                facing = None
+                for axis in range(3):
+                    offset = listen_ref[axis : axis + 1, lanes] - columns[rows, axis : axis + 1]
+                    square = offset * offset
+                    along = columns[rows, axis + 3 : axis + 4] * offset
+                    distance_sq = square if distance_sq is None else distance_sq + square
+                    facing = along if facing is None else facing + along
+                distance = jnp.sqrt(distance_sq)
+                far = facing / (4.0 * math.pi * sound_speed * distance_sq)
+                angle = angle_step * distance
+                turn = jnp.cos(angle)
+                at = owner * (P_OWN // 8) + group
+                wave_ref[tile, at, 0] = far
+                wave_ref[tile, at, 1] = jnp.zeros_like(far)
+                wave_ref[tile, at, 2] = far * turn
+                wave_ref[tile, at, 3] = far * jnp.sin(angle)
+                wave_ref[tile, at, 4] = 2.0 * turn
+                wave_ref[tile, at, 5] = sound_speed / distance
+
+        for group in range(P_OWN // 8):
+            one_group(group)
+
+
+def spread_panels(panel_ref, wide_ref, first):
+    groups, count = wide_ref.shape[0], wide_ref.shape[1]
+    together = 4
+
+    def some_groups(index, carry):
+        at = index * together
+        panels = [
+            panel_ref[pl.ds(pl.multiple_of((at + step) * 8, 8), 8), :] for step in range(together)
+        ]
+        for part in range(4):
+            for number in range(count):
+                column = part * BINS + first + number
+                for step in range(together):
+                    wide_ref[at + step, number, part] = jnp.broadcast_to(
+                        panels[step][:, column : column + 1], (8, LANES)
+                    )
+        return carry
+
+    lax.fori_loop(0, groups // together, some_groups, 0)
+
+
+def radiate_tile(wave_ref, panel_ref, wide_ref, sums_ref, total_ref):
+    groups = wave_ref.shape[0]
+    held = wide_ref.shape[1]
+    span = 8
+    unroll = 4
+    for first in range(0, BINS, span):
+        if held < BINS and first % held == 0:
+            spread_panels(panel_ref, wide_ref, first)
+
+        def add_groups(index, sums, first=first):
+            sums = list(sums)
+            for step in range(unroll):
+                at = index * unroll + step
+                old_cos, old_sin, now_cos, now_sin, twice, ratio = [wave_ref[at, i] for i in range(6)]
+                for number in range(span):
+                    k = first + number
+                    press_real, press_imag, rate_real, rate_imag = [
+                        wide_ref[at, k % held, part] for part in range(4)
+                    ]
+                    mixed_real = rate_real + ratio * press_real
+                    mixed_imag = rate_imag + ratio * press_imag
+                    real = mixed_real * now_cos + mixed_imag * now_sin
+                    imag = mixed_imag * now_cos - mixed_real * now_sin
+                    sums[number] = sums[number] + real
+                    sums[span + number] = sums[span + number] + imag
+                    if k + 1 < BINS:
+                        old_cos, now_cos = now_cos, twice * now_cos - old_cos
+                        old_sin, now_sin = now_sin, twice * now_sin - old_sin
+                if first + span < BINS:
+                    for i, value in enumerate([old_cos, old_sin, now_cos, now_sin]):
+                        wave_ref[at, i] = value
+            return tuple(sums)
+
+        blank = jnp.zeros((8, LANES), jnp.float32)
+        sums = lax.fori_loop(0, groups // unroll, add_groups, (blank,) * (2 * span))
+        for number in range(span):
+            k = first + number
+            sums_ref[k * 8 : (k + 1) * 8, :] = sums[number]
+            sums_ref[(BINS + k) * 8 : (BINS + k + 1) * 8, :] = sums[span + number]
+    total = sums_ref[pl.ds(0, 2 * BINS, stride=8), :]
+    for row in range(1, 8):
+        total = total + sums_ref[pl.ds(row, 2 * BINS, stride=8), :]
+    total_ref[...] = total
+
+
 def window_kernel(
-    blocks, ring, face_ref, rim_face_ref, count_ref, start_ref, owner_ref, probe_ref, history_ref,
-    place_ref, normal_ref, table_ref, tail_ref, field_ref, spectra_ref, place_out_ref,
-    density_ref, rolled_ref, moving_ref, edge_ref, near_ref, draft_ref, piece_ref,
+    blocks, ring, face_ref, rim_face_ref, count_ref, start_hbm, owner_ref, probe_ref, history_ref,
+    place_ref, normal_ref, listen_ref, table_ref, tail_ref, final_hbm, out_ref,
+    field_ref, density_ref, rolled_ref, moving_ref, edge_ref, near_ref, draft_ref, piece_ref,
     send_ref, got_even, got_odd, select_ref, cell_ref, past_send, past_got, flat_ref, choose_ref,
     partial_ref, fresh_ref, fresh_send, fresh_got, fresh_flat, done_ref, done_got, spot_ref, spot_got,
+    wave_ref, panel_ref, wide_ref, sums_ref, total_ref, part_send, part_got,
     edge_send, edge_got, send_sem, got_sem, past_send_sem, past_got_sem, fresh_send_sem, fresh_got_sem,
     done_send_sem, done_got_sem, spot_send_sem, spot_got_sem,
+    part_send_sem, part_got_sem, local_sem,
 ):
     mesh_ids = pl.DeviceIdType.MESH
     me = lax.axis_index("blk")
@@ -369,14 +472,16 @@
     lax.fori_loop(1, blocks, greet, 0)
     face = [face_ref[0, k] for k in range(4)]
     edge = [rim_face_ref[0, k] for k in range(4)]
-    field_ref[...] = start_ref[...]
+    load = pltpu.make_async_copy(start_hbm, field_ref, local_sem.at[0])
+    load.start()
     route(blocks, owner_ref, count_ref[0], history_ref, select_ref, past_send)
-    cell = lax.rem(probe_ref[...], start_ref.shape[2])
+    cell = lax.rem(probe_ref[...], field_ref.shape[2])
     cell_ref[...] = jnp.where(rows_of(cell_ref.shape) == cell, 1.0, 0.0).astype(jnp.bfloat16)
     spot_ref[...] = jnp.zeros_like(spot_ref)
     spot_ref[0:3, 0:P_OWN] = place_ref[...].astype(jnp.float32)
     spot_ref[3:6, 0:P_OWN] = normal_ref[...].astype(jnp.float32)
     fresh_ref[...] = jnp.zeros_like(fresh_ref)
+    load.wait()
 
     def swap(source_of, into_ref, send_sems, got_sems, distance):
         peer = lax.rem(me + distance, blocks)
@@ -466,8 +571,13 @@
             for copy in ring_copies(spot_ref, spot_got, spot_send_sem, spot_got_sem):
                 copy.start()
             past_got[me] = past_send[me]
+            spot_got[side] = spot_ref[...]
         else:
             note(step - 1)
+        if step == 1:
+            for copy in ring_copies(spot_ref, spot_got, spot_send_sem, spot_got_sem):
+                copy.wait()
+            prepare_waves(spot_got, listen_ref, wave_ref)
         if step == 2:
             every(lambda distance: past_copy(distance).wait())
             settle_history(past_got, flat_ref, choose_ref, table_ref, partial_ref)
@@ -476,6 +586,8 @@
 
     for step in range(STEPS):
         one_step(step)
+    unload = pltpu.make_async_copy(field_ref, final_hbm, local_sem.at[1])
+    unload.start()
     note(STEPS - 1)
     fresh = joined(select_ref[...], fresh_ref[...], 1, 1)
     room = fresh_send.shape[1]
@@ -483,10 +595,6 @@
         fresh_send[block] = fresh[block * room : (block + 1) * room].astype(jnp.bfloat16)
     every(lambda distance: fresh_copy(distance).start())
     fresh_got[me] = fresh_send[me]
-    for copy in ring_copies(spot_ref, spot_got, spot_send_sem, spot_got_sem):
-        copy.wait()
-    spot_got[side] = spot_ref[...]
-    place_out_ref[...] = spot_got[...]
     every(lambda distance: fresh_copy(distance).wait())
     unpacked(fresh_got, fresh_flat)
     newest = joined(choose_ref[...], fresh_flat[...], 0, 0)
@@ -498,7 +606,49 @@
     done_got[side] = done_ref[...]
     for copy in copies:
         copy.wait()
-    spectra_ref[...] = done_got[...].astype(jnp.float32)
+    for owner in range(ring):
+        panel_ref[owner * P_OWN : (owner + 1) * P_OWN, :] = done_got[owner].astype(jnp.float32)
+    if wide_ref.shape[1] == BINS:
+        spread_panels(panel_ref, wide_ref, 0)
+    chunk = out_ref.shape[0]
+    tiles = wave_ref.shape[0]
+    share = LANES // chunk
+
+    def part_copy(peer):
+        distance = lax.rem(peer - me + blocks, blocks)
+        return pltpu.make_async_remote_copy(
+            src_ref=part_send.at[peer],
+            dst_ref=part_got.at[me],
+            send_sem=part_send_sem.at[distance],
+            recv_sem=part_got_sem.at[distance],
+            device_id=(peer, side),
+            device_id_type=mesh_ids,
+        )
+
+    def one_tile(turn, carry):
+        tile = lax.rem(me // share + 1 + turn, tiles)
+        radiate_tile(wave_ref.at[tile], panel_ref, wide_ref, sums_ref, total_ref)
+        both = total_ref[...].T
+        for number in range(share):
+            part_send[tile * share + number] = both[number * chunk : (number + 1) * chunk]
+
+        def launch(number, inner):
+            peer = tile * share + number
+
+            @pl.when(peer != me)
+            def _():
+                part_copy(peer).start()
+
+            return inner
+
+        lax.fori_loop(0, share, launch, 0)
+        return carry
+
+    lax.fori_loop(0, tiles, one_tile, 0)
+    part_got[me] = part_send[me]
+    every(lambda distance: part_copy(lax.rem(me + distance, blocks)).wait())
+    out_ref[...] = jnp.sum(part_got[...], axis=0)
+    unload.wait()
 
 
 def transform_tables():
@@ -514,108 +664,6 @@
         rows = slice(field * STEPS, (field + 1) * STEPS)
         tail[rows, field * 2 * BINS : (field + 1) * 2 * BINS] = table[SAMPLES - STEPS :]
     return jnp.asarray(past), jnp.asarray(tail)
-
-
-def greet_peers(blocks):
-    me = lax.axis_index("blk")
-    side = lax.axis_index("obs")
-    barrier = pltpu.get_barrier_semaphore()
-
-    def greet(distance, carry):
-        pl.semaphore_signal(
-            barrier, inc=1, device_id=(lax.rem(me + distance, blocks), side),
-            device_id_type=pl.DeviceIdType.MESH,
-        )
-        return carry
-
-    lax.fori_loop(1, blocks, greet, 0)
-    return barrier
-
-
-def swap_pieces(blocks, send_ref, got_ref, send_sem, got_sem):
-    me = lax.axis_index("blk")
-    side = lax.axis_index("obs")
-
-    def copy_to(distance):
-        peer = lax.rem(me + distance, blocks)
-        return pltpu.make_async_remote_copy(
-            src_ref=send_ref.at[peer],
-            dst_ref=got_ref.at[me],
-            send_sem=send_sem.at[distance],
-            recv_sem=got_sem.at[distance],
-            device_id=(peer, side),
-            device_id_type=pl.DeviceIdType.MESH,
-        )
-
-    def begin(distance, inner):
-        copy_to(distance).start()
-        return inner
-
-    def finish(distance, inner):
-        copy_to(distance).wait()
-        return inner
-
-    lax.fori_loop(1, blocks, begin, 0)
-    lax.fori_loop(1, blocks, finish, 0)
-
-
-def radiate_kernel(
-    blocks, panel_ref, listen_ref, out_ref,
-    real_ref, imag_ref, full_ref, send_ref, got_ref, send_sem, got_sem,
-):
-    barrier = greet_peers(blocks)
-    listeners = listen_ref.shape[1]
-    real_ref[...] = jnp.zeros_like(real_ref)
-    imag_ref[...] = jnp.zeros_like(imag_ref)
-    step_angle = 2.0 * math.pi / SAMPLES / sound_speed
-
-    def accumulate(block_number, carry):
-        begin = pl.multiple_of(block_number * 8, 8)
-        panel = panel_ref[pl.ds(begin, 8), :]
-        distance_sq = None
-        facing = None
-        for axis in range(3):
-            at = 4 * BINS + axis
-            offset = listen_ref[axis : axis + 1, :] - panel[:, at : at + 1]
-            square = offset * offset
-            along = panel[:, at + 3 : at + 4] * offset
-            distance_sq = square if distance_sq is None else distance_sq + square
-            facing = along if facing is None else facing + along
-        distance = jnp.sqrt(distance_sq)
-        far_term = facing / (4.0 * math.pi * sound_speed * distance_sq)
-        ratio = sound_speed / distance
-        angle = step_angle * distance
-        turn_cos = jnp.cos(angle)
-        turn_sin = jnp.sin(angle)
-        wave_cos = far_term * turn_cos
-        wave_sin = far_term * turn_sin
-        for k in range(BINS):
-            press_real = panel[:, k : k + 1]
-            press_imag = panel[:, BINS + k : BINS + k + 1]
-            rate_real = panel[:, 2 * BINS + k : 2 * BINS + k + 1]
-            rate_imag = panel[:, 3 * BINS + k : 3 * BINS + k + 1]
-            mixed_real = rate_real + ratio * press_real
-            mixed_imag = rate_imag + ratio * press_imag
-            real_ref[k] += mixed_real * wave_cos + mixed_imag * wave_sin
-            imag_ref[k] += mixed_imag * wave_cos - mixed_real * wave_sin
-            if k + 1 < BINS:
-                wave_cos, wave_sin = (
-                    wave_cos * turn_cos - wave_sin * turn_sin,
-                    wave_sin * turn_cos + wave_cos * turn_sin,
-                )
-        return carry
-
-    lax.fori_loop(0, panel_ref.shape[0] // 8, accumulate, 0)
-    both = jnp.concatenate([jnp.sum(real_ref[...], axis=1), jnp.sum(imag_ref[...], axis=1)], axis=0)
-    full_ref[...] = both.T
-    chunk = out_ref.shape[0]
-    for number in range(blocks):
-        send_ref[number] = full_ref[number * chunk : (number + 1) * chunk]
-    me = lax.axis_index("blk")
-    got_ref[me] = send_ref[me]
-    pl.semaphore_wait(barrier, blocks - 1)
-    swap_pieces(blocks, send_ref, got_ref, send_sem, got_sem)
-    out_ref[...] = jnp.sum(got_ref[...], axis=0)
 
 
 def body(
@@ -638,22 +686,26 @@
     tiles = lane_count // LANES
     vmem = pl.BlockSpec(memory_space=pltpu.VMEM)
     smem = pl.BlockSpec(memory_space=pltpu.SMEM)
+    anywhere = pl.BlockSpec(memory_space=pl.ANY)
     wide = jnp.float32
     half = jnp.bfloat16
     slots = panel_owner.shape[0]
     room = -(-slots // blocks)
     past, tail = transform_tables()
     dma = pltpu.SemaphoreType.DMA
-    lattice_state, spectra, places = pl.pallas_call(
+    listeners = observers.shape[1]
+    chunk = listeners // blocks
+    held = BINS if ring * P_OWN <= 2 * LANES else BINS // 4
+    lattice_state, spectrum = pl.pallas_call(
         functools.partial(window_kernel, blocks, ring),
         out_shape=[
             jax.ShapeDtypeStruct((19, slab_depth, lane_count), wide),
-            jax.ShapeDtypeStruct((ring, P_OWN, 4 * BINS), wide),
-            jax.ShapeDtypeStruct((ring, 8, LANES), wide),
+            jax.ShapeDtypeStruct((chunk, 2 * BINS), wide),
         ],
-        in_specs=[smem] * 3 + [vmem] * 8,
-        out_specs=[vmem] * 3,
+        in_specs=[smem] * 3 + [anywhere] + [vmem] * 8,
+        out_specs=[anywhere, vmem],
         scratch_shapes=[
+            pltpu.VMEM((19, slab_depth, lane_count), wide),
             pltpu.VMEM((STEPS, slab_depth, lane_count), wide),
             pltpu.VMEM((tiles + 2, 19, slab_depth, LANES), wide),
             pltpu.VMEM((tiles, len(x_order), slab_depth, LANES), wide),
@@ -679,36 +731,26 @@
             pltpu.VMEM((ring, P_OWN, 4 * BINS), half),
             pltpu.VMEM((8, LANES), wide),
             pltpu.VMEM((ring, 8, LANES), wide),
+            pltpu.VMEM((listeners // LANES, ring * P_OWN // 8, 6, 8, LANES), wide),
+            pltpu.VMEM((ring * P_OWN, 4 * BINS), wide),
+            pltpu.VMEM((ring * P_OWN // 8, held, 4, 8, LANES), wide),
+            pltpu.VMEM((2 * BINS * 8, LANES), wide),
+            pltpu.VMEM((2 * BINS, LANES), wide),
+            pltpu.VMEM((blocks, chunk, 2 * BINS), wide),
+            pltpu.VMEM((blocks, chunk, 2 * BINS), wide),
         ]
         + [dma((STEPS, 2))] * 2
         + [dma((STEPS, blocks))] * 2
         + [dma((blocks,))] * 4
-        + [dma((ring,))] * 4,
+        + [dma((ring,))] * 4
+        + [dma((blocks,))] * 2
+        + [dma((2,))],
         compiler_params=pltpu.CompilerParams(collective_id=0, has_side_effects=True),
     )(
         block_faces, block_edges, panel_count, lattice_state, panel_owner[None], probe_cell[None],
-        history, panel_pos, panel_normal, past, tail,
+        history, panel_pos, panel_normal, observers, past, tail,
     )
     populations_out = lattice_state.reshape(1, 19, slab_depth, lane_count)
-    places = places[:, :, :P_OWN].transpose(0, 2, 1).reshape(ring * P_OWN, 8)
-    gathered = jnp.concatenate([spectra.reshape(ring * P_OWN, 4 * BINS), places], axis=1)
-    listeners = observers.shape[1]
-    chunk = listeners // blocks
-    spectrum = pl.pallas_call(
-        functools.partial(radiate_kernel, blocks),
-        out_shape=jax.ShapeDtypeStruct((chunk, 2 * BINS), jnp.float32),
-        in_specs=[vmem, vmem],
-        out_specs=vmem,
-        scratch_shapes=[
-            pltpu.VMEM(shape, jnp.float32)
-            for shape in [
-                (BINS, 8, listeners), (BINS, 8, listeners), (listeners, 2 * BINS),
-                (blocks, chunk, 2 * BINS), (blocks, chunk, 2 * BINS),
-            ]
-        ]
-        + [pltpu.SemaphoreType.DMA((blocks,))] * 2,
-        compiler_params=pltpu.CompilerParams(collective_id=2, has_side_effects=True),
-    )(gathered, observers)
     return (populations_out, spectrum[None])
 
 

time: 78.1 us -> 73.4 us (0.940)
  Pallas kernels: 71.1 us -> 68.8 us
  other arithmetic: 1.6 us -> 0 us
  local copies, waits for them, and re-layouts: 3.87 us -> 3.08 us
    pallas_call x1 -> x0, Pallas kernels: 23.3 us -> none  [body(): pl.pallas_call(functools.partial(radiate_kernel, blocks), out_shape=jax.S...]
    pallas_call x1, Pallas kernels: 47.8 us -> 68.8 us  [body(): pl.pallas_call(functools.partial(window_kernel, blocks, ring), out_shape=...]
    concatenate x1 -> x0, other arithmetic: 1.6 us -> none  [body(): jnp.concatenate([spectra.reshape(ring * P_OWN, 4 * BINS), places], axis=1)]
    transpose x2 -> x0, local copies, waits for them, and re-layouts: 0.79 us -> none  [body(): places = places[:, :, :P_OWN].transpose(0, 2, 1).reshape(ring * P_OWN, 8)]
where the time goes in v3:
time: 73.4 us; the launch traced here: 73.2 us
  Pallas kernels  68.8 us (94%)
  local copies, waits for them, and re-layouts  3.08 us (4%)
  between operations  1.3 us (2%)
    pallas_call x1, Pallas kernels, body(): pl.pallas_call(functools.partial(window_kernel, blocks, ring), out_shape=...  68.8 us
    unnamed x4, local copies, waits for them, and re-layouts  3.08 us

profile of v3, /device:TPU:0, one launch (start us, length us, event | category | flops | bytes accessed | tf_op | source)
XLA Modules:
  0.0 73.2 jit_solution(9525040228560546646)
XLA Ops:
  1.3 68.8 %shard_map.131 = (f32[19,16,1024]{2,1,0:T(8,128)}, f32[32,128]{1,0:T(8,128)}) custom-call(s32[1,4]{1,0:T(1,128)} %face_ref.1, s32[1,4]{1,0:T(1,128)} %rim_face_ref.1, s32[1]{0:T(128)S(6)} %copy.16.count_ref, f32[19,16,1024]{2,1,0:T(8,128)} %bitcast.6, s32[1,128]{1,0:T(1,128)} %bitcast.8, s32[1,128]{1,0:T(1,128)} %bitcast.9, bf16[128,512]{1,0:T(8,128)(2,1)} %history_ref.1, ...), custom_call_target="tpu_custom_call" | custom-call | tf_op jit(solution)/shard_map/pallas_call | solution.py:699
  70.1 0.0 copy-start
  70.1 2.5 %copy.17 = f32[1,19,16,1024]{3,2,1,0:T(8,128)} copy(f32[1,19,16,1024]{3,2,1,0:T(8,128)} %bitcast.5) | data formatting | bytes 2490368
  72.6 0.0 copy-done
  72.6 0.6 copy.18
Async XLA Ops:
  70.1 2.5 %copy-start = (f32[32,128]{1,0:T(8,128)S(1)}, f32[32,128]{1,0:T(8,128)}, u32[]{:S(2)}) copy-start(f32[32,128]{1,0:T(8,128)} %get-tuple-element.5) | copy-start | bytes 49156

commit v4 on v3

--- a/solution.py
+++ b/solution.py
@@ -343,15 +343,15 @@
 
 def prepare_waves(spot_got, listen_ref, wave_ref):
     ring = spot_got.shape[0]
-    tiles = wave_ref.shape[0]
+    tiles, width = wave_ref.shape[0], wave_ref.shape[3]
     angle_step = 2.0 * math.pi / SAMPLES / sound_speed
     for owner in range(ring):
-        columns = spot_got[owner].T
-
-        def one_group(group, columns=columns):
+        columns = spot_got[owner].T[0:P_OWN]
+        for group in range(P_OWN // 8):
             rows = slice(group * 8, (group + 1) * 8)
+            into = slice(owner * P_OWN + group * 8, owner * P_OWN + (group + 1) * 8)
             for tile in range(tiles):
-                lanes = slice(tile * LANES, (tile + 1) * LANES)
+                lanes = slice(tile * width, (tile + 1) * width)
                 distance_sq = None
                 facing = None
                 for axis in range(3):
@@ -364,82 +364,62 @@
                 far = facing / (4.0 * math.pi * sound_speed * distance_sq)
                 angle = angle_step * distance
                 turn = jnp.cos(angle)
-                at = owner * (P_OWN // 8) + group
-                wave_ref[tile, at, 0] = far
-                wave_ref[tile, at, 1] = jnp.zeros_like(far)
-                wave_ref[tile, at, 2] = far * turn
-                wave_ref[tile, at, 3] = far * jnp.sin(angle)
-                wave_ref[tile, at, 4] = 2.0 * turn
-                wave_ref[tile, at, 5] = sound_speed / distance
-
-        for group in range(P_OWN // 8):
-            one_group(group)
-
-
-def spread_panels(panel_ref, wide_ref, first):
-    groups, count = wide_ref.shape[0], wide_ref.shape[1]
-    together = 4
-
-    def some_groups(index, carry):
-        at = index * together
-        panels = [
-            panel_ref[pl.ds(pl.multiple_of((at + step) * 8, 8), 8), :] for step in range(together)
-        ]
-        for part in range(4):
-            for number in range(count):
-                column = part * BINS + first + number
-                for step in range(together):
-                    wide_ref[at + step, number, part] = jnp.broadcast_to(
-                        panels[step][:, column : column + 1], (8, LANES)
-                    )
-        return carry
-
-    lax.fori_loop(0, groups // together, some_groups, 0)
-
-
-def radiate_tile(wave_ref, panel_ref, wide_ref, sums_ref, total_ref):
-    groups = wave_ref.shape[0]
-    held = wide_ref.shape[1]
-    span = 8
-    unroll = 4
+                wave_ref[tile, 0, into] = far
+                wave_ref[tile, 1, into] = jnp.zeros_like(far)
+                wave_ref[tile, 2, into] = far * turn
+                wave_ref[tile, 3, into] = far * jnp.sin(angle)
+                wave_ref[tile, 4, into] = 2.0 * turn
+                wave_ref[tile, 5, into] = sound_speed / distance
+
+
+def weigh_panels(done_got, weight_ref):
+    ring = done_got.shape[0]
+    panels = ring * P_OWN
+    values = jnp.concatenate([done_got[owner].astype(jnp.float32) for owner in range(ring)], axis=0).T
+    press_real, press_imag, rate_real, rate_imag = [
+        values[part * BINS : (part + 1) * BINS] for part in range(4)
+    ]
+    lines = [
+        [rate_real, rate_imag, press_real, press_imag],
+        [rate_imag, -rate_real, press_imag, -press_real],
+    ]
+    for row, line in enumerate(lines):
+        for part, value in enumerate(line):
+            for start in range(0, panels, LANES):
+                at = (part * panels + start) // LANES
+                weight_ref[at, pl.ds(row, BINS, stride=8), :] = value[:, start : start + LANES]
+
+
+def radiate_tile(wave_ref, weight_ref, first_ref, second_ref, sums_ref, total_ref):
+    panels = wave_ref.shape[1]
+    span = first_ref.shape[0]
     for first in range(0, BINS, span):
-        if held < BINS and first % held == 0:
-            spread_panels(panel_ref, wide_ref, first)
-
-        def add_groups(index, sums, first=first):
-            sums = list(sums)
-            for step in range(unroll):
-                at = index * unroll + step
-                old_cos, old_sin, now_cos, now_sin, twice, ratio = [wave_ref[at, i] for i in range(6)]
-                for number in range(span):
-                    k = first + number
-                    press_real, press_imag, rate_real, rate_imag = [
-                        wide_ref[at, k % held, part] for part in range(4)
-                    ]
-                    mixed_real = rate_real + ratio * press_real
-                    mixed_imag = rate_imag + ratio * press_imag
-                    real = mixed_real * now_cos + mixed_imag * now_sin
-                    imag = mixed_imag * now_cos - mixed_real * now_sin
-                    sums[number] = sums[number] + real
-                    sums[span + number] = sums[span + number] + imag
-                    if k + 1 < BINS:
-                        old_cos, now_cos = now_cos, twice * now_cos - old_cos
-                        old_sin, now_sin = now_sin, twice * now_sin - old_sin
-                if first + span < BINS:
-                    for i, value in enumerate([old_cos, old_sin, now_cos, now_sin]):
-                        wave_ref[at, i] = value
-            return tuple(sums)
-
-        blank = jnp.zeros((8, LANES), jnp.float32)
-        sums = lax.fori_loop(0, groups // unroll, add_groups, (blank,) * (2 * span))
+        held_ref = second_ref if first // span % 2 else first_ref
+        for start in range(0, panels, 32):
+            rows = slice(start, start + 32)
+            old_cos, old_sin, now_cos, now_sin, twice, ratio = [wave_ref[i, rows] for i in range(6)]
+            for number in range(span):
+                near = [now_cos, now_sin, ratio * now_cos, ratio * now_sin]
+                for part, value in enumerate(near):
+                    into = slice(part * panels + start, part * panels + start + 32)
+                    held_ref[number, into] = value.astype(jnp.bfloat16)
+                if first + number + 1 < BINS:
+                    old_cos, now_cos = now_cos, twice * now_cos - old_cos
+                    old_sin, now_sin = now_sin, twice * now_sin - old_sin
+            if first + span < BINS:
+                for i, value in enumerate([old_cos, old_sin, now_cos, now_sin]):
+                    wave_ref[i, rows] = value
         for number in range(span):
-            k = first + number
-            sums_ref[k * 8 : (k + 1) * 8, :] = sums[number]
-            sums_ref[(BINS + k) * 8 : (BINS + k + 1) * 8, :] = sums[span + number]
-    total = sums_ref[pl.ds(0, 2 * BINS, stride=8), :]
-    for row in range(1, 8):
-        total = total + sums_ref[pl.ds(row, 2 * BINS, stride=8), :]
-    total_ref[...] = total
+            rows = slice((first + number) * 8, (first + number + 1) * 8)
+            weights = jnp.concatenate(
+                [weight_ref[at, rows, :] for at in range(weight_ref.shape[0])], axis=1
+            )
+            found = joined(weights, held_ref[number], 1, 0)
+            for part in range(sums_ref.shape[0]):
+                sums_ref[part, rows, :] = found[:, part * LANES : (part + 1) * LANES]
+    for part in range(sums_ref.shape[0]):
+        total_ref[part, 0:BINS] = sums_ref[part, pl.ds(0, BINS, stride=8), :]
+        total_ref[part, BINS : 2 * BINS] = sums_ref[part, pl.ds(1, BINS, stride=8), :]
 
 
 def window_kernel(
@@ -448,7 +428,7 @@
     field_ref, density_ref, rolled_ref, moving_ref, edge_ref, near_ref, draft_ref, piece_ref,
     send_ref, got_even, got_odd, select_ref, cell_ref, past_send, past_got, flat_ref, choose_ref,
     partial_ref, fresh_ref, fresh_send, fresh_got, fresh_flat, done_ref, done_got, spot_ref, spot_got,
-    wave_ref, panel_ref, wide_ref, sums_ref, total_ref, part_send, part_got,
+    wave_ref, weight_ref, first_ref, second_ref, sums_ref, total_ref, part_send, part_got,
     edge_send, edge_got, send_sem, got_sem, past_send_sem, past_got_sem, fresh_send_sem, fresh_got_sem,
     done_send_sem, done_got_sem, spot_send_sem, spot_got_sem,
     part_send_sem, part_got_sem, local_sem,
@@ -606,13 +586,10 @@
     done_got[side] = done_ref[...]
     for copy in copies:
         copy.wait()
-    for owner in range(ring):
-        panel_ref[owner * P_OWN : (owner + 1) * P_OWN, :] = done_got[owner].astype(jnp.float32)
-    if wide_ref.shape[1] == BINS:
-        spread_panels(panel_ref, wide_ref, 0)
+    weigh_panels(done_got, weight_ref)
     chunk = out_ref.shape[0]
     tiles = wave_ref.shape[0]
-    share = LANES // chunk
+    share = wave_ref.shape[3] // chunk
 
     def part_copy(peer):
         distance = lax.rem(peer - me + blocks, blocks)
@@ -627,10 +604,13 @@
 
     def one_tile(turn, carry):
         tile = lax.rem(me // share + 1 + turn, tiles)
-        radiate_tile(wave_ref.at[tile], panel_ref, wide_ref, sums_ref, total_ref)
-        both = total_ref[...].T
-        for number in range(share):
-            part_send[tile * share + number] = both[number * chunk : (number + 1) * chunk]
+        radiate_tile(wave_ref.at[tile], weight_ref, first_ref, second_ref, sums_ref, total_ref)
+        each = LANES // chunk
+        for part in range(total_ref.shape[0]):
+            both = total_ref[part].T
+            for number in range(each):
+                rows = slice(number * chunk, (number + 1) * chunk)
+                part_send[tile * share + part * each + number] = both[rows]
 
         def launch(number, inner):
             peer = tile * share + number
@@ -695,7 +675,7 @@
     dma = pltpu.SemaphoreType.DMA
     listeners = observers.shape[1]
     chunk = listeners // blocks
-    held = BINS if ring * P_OWN <= 2 * LANES else BINS // 4
+    width = min(2 * LANES, listeners)
     lattice_state, spectrum = pl.pallas_call(
         functools.partial(window_kernel, blocks, ring),
         out_shape=[
@@ -731,11 +711,12 @@
             pltpu.VMEM((ring, P_OWN, 4 * BINS), half),
             pltpu.VMEM((8, LANES), wide),
             pltpu.VMEM((ring, 8, LANES), wide),
-            pltpu.VMEM((listeners // LANES, ring * P_OWN // 8, 6, 8, LANES), wide),
-            pltpu.VMEM((ring * P_OWN, 4 * BINS), wide),
-            pltpu.VMEM((ring * P_OWN // 8, held, 4, 8, LANES), wide),
-            pltpu.VMEM((2 * BINS * 8, LANES), wide),
-            pltpu.VMEM((2 * BINS, LANES), wide),
+            pltpu.VMEM((listeners // width, 6, ring * P_OWN, width), wide),
+            pltpu.VMEM((4 * ring * P_OWN // LANES, BINS * 8, LANES), wide),
+            pltpu.VMEM((8, 4 * ring * P_OWN, width), half),
+            pltpu.VMEM((8, 4 * ring * P_OWN, width), half),
+            pltpu.VMEM((width // LANES, BINS * 8, LANES), wide),
+            pltpu.VMEM((width // LANES, 2 * BINS, LANES), wide),
             pltpu.VMEM((blocks, chunk, 2 * BINS), wide),
             pltpu.VMEM((blocks, chunk, 2 * BINS), wide),
         ]

time: 73.4 us -> 63.7 us (0.87)
  Pallas kernels: 68.8 us -> 59.1 us
    pallas_call x1, Pallas kernels: 68.8 us -> 59.1 us  [body(): pl.pallas_call(functools.partial(window_kernel, blocks, ring), out_shape=...]
where the time goes in v4:
time: 63.7 us; the launch traced here: 63.4 us
  Pallas kernels  59.1 us (93%)
  local copies, waits for them, and re-layouts  3.08 us (5%)
  between operations  1.3 us (2%)
    pallas_call x1, Pallas kernels, body(): pl.pallas_call(functools.partial(window_kernel, blocks, ring), out_shape=...  59.1 us
    unnamed x4, local copies, waits for them, and re-layouts  3.08 us

profile of v4, /device:TPU:0, one launch (start us, length us, event | category | flops | bytes accessed | tf_op | source)
XLA Modules:
  0.0 63.4 jit_solution(15731563284011445696)
XLA Ops:
  1.3 59.1 %shard_map.131 = (f32[19,16,1024]{2,1,0:T(8,128)}, f32[32,128]{1,0:T(8,128)}) custom-call(s32[1,4]{1,0:T(1,128)} %face_ref.1, s32[1,4]{1,0:T(1,128)} %rim_face_ref.1, s32[1]{0:T(128)S(6)} %copy.16.count_ref, f32[19,16,1024]{2,1,0:T(8,128)} %bitcast.6, s32[1,128]{1,0:T(1,128)} %bitcast.8, s32[1,128]{1,0:T(1,128)} %bitcast.9, bf16[128,512]{1,0:T(8,128)(2,1)} %history_ref.1, ...), custom_call_target="tpu_custom_call" | custom-call | tf_op jit(solution)/shard_map/pallas_call | solution.py:679
  60.4 0.0 copy-start
  60.4 2.5 %copy.17 = f32[1,19,16,1024]{3,2,1,0:T(8,128)} copy(f32[1,19,16,1024]{3,2,1,0:T(8,128)} %bitcast.5) | data formatting | bytes 2490368
  62.8 0.0 copy-done
  62.8 0.6 copy.18
Async XLA Ops:
  60.4 2.5 %copy-start = (f32[32,128]{1,0:T(8,128)S(1)}, f32[32,128]{1,0:T(8,128)}, u32[]{:S(2)}) copy-start(f32[32,128]{1,0:T(8,128)} %get-tuple-element.5) | copy-start | bytes 49156

commit v5 on v4

--- a/solution.py
+++ b/solution.py
@@ -154,7 +154,7 @@
                 rows[side][j // 4] = jnp.where(quarter == j % 4, moved, rows[side][j // 4])
 
 
-def collide_all(field_ref, rolled_ref, moving_ref, edge_ref, draft_ref):
+def collide_all(field_ref, rolled_ref, moving_ref, draft_ref):
     depth = field_ref.shape[1]
     tiles = field_ref.shape[2] // LANES
     blank = jnp.zeros((depth, LANES), jnp.float32)
@@ -170,16 +170,28 @@
                     rolled_ref[tile + 1, number] = turned(out[number], shift_of(number))
                 else:
                     moving_ref[tile, x_order.index(number)] = out[number]
-            for place, number in enumerate(x_plus):
-                edge_ref[0, place, tile : tile + 1, :] = out[number][depth - 1 : depth]
-            for place, number in enumerate(x_minus):
-                edge_ref[1, place, tile : tile + 1, :] = out[number][0:1]
             pack_tile(out, tile, tiles, still, columns, rows)
         for side in range(2):
             draft_ref[2 + side, :, half * LANES : (half + 1) * LANES] = columns[side]
     for side in range(2):
         for half in range(2):
             draft_ref[side, :, half * LANES : (half + 1) * LANES] = rows[side][half]
+
+
+def keep_rim(rim_ref, number, tile, value):
+    depth = value.shape[0]
+    tiles = rim_ref.shape[1] // 2
+    rim_ref[number, tile : tile + 1, :] = value[depth - 1 : depth]
+    rim_ref[number, tiles + tile : tiles + tile + 1, :] = value[0:1]
+
+
+def collide_rim(rim_ref, edge_ref):
+    tiles = rim_ref.shape[1] // 2
+    out = collide_tile([rim_ref[number] for number in range(19)])
+    for place, number in enumerate(x_plus):
+        edge_ref[0, place] = out[number][0:tiles]
+    for place, number in enumerate(x_minus):
+        edge_ref[1, place] = out[number][tiles : 2 * tiles]
 
 
 def shifted(moving_ref, near_ref, tile, number):
@@ -221,7 +233,7 @@
             rolled_ref[tile + 1, number] = turned(value, shift_of(number))
 
 
-def finish_step(face, edge, got_ref, rolled_ref, field_ref, density_ref):
+def finish_step(face, edge, got_ref, rolled_ref, field_ref, rim_ref, density_ref, last):
     depth = field_ref.shape[1]
     tiles = field_ref.shape[2] // LANES
     lane = lane_of((depth, LANES))
@@ -270,6 +282,8 @@
                 elif shift_y == -1:
                     value = jnp.where(lane >= LANES - BS, rolled_ref[tile + 2, number], value)
                 field_ref[number, :, lanes] = value
+            if not last:
+                keep_rim(rim_ref, number, tile, value)
             total = value if total is None else total + value
         density_ref[:, lanes] = total
 
@@ -425,7 +439,7 @@
 def window_kernel(
     blocks, ring, face_ref, rim_face_ref, count_ref, start_hbm, owner_ref, probe_ref, history_ref,
     place_ref, normal_ref, listen_ref, table_ref, tail_ref, final_hbm, out_ref,
-    field_ref, density_ref, rolled_ref, moving_ref, edge_ref, near_ref, draft_ref, piece_ref,
+    field_ref, density_ref, rolled_ref, moving_ref, rim_ref, edge_ref, near_ref, draft_ref, piece_ref,
     send_ref, got_even, got_odd, select_ref, cell_ref, past_send, past_got, flat_ref, choose_ref,
     partial_ref, fresh_ref, fresh_send, fresh_got, fresh_flat, done_ref, done_got, spot_ref, spot_got,
     wave_ref, weight_ref, first_ref, second_ref, sums_ref, total_ref, part_send, part_got,
@@ -462,6 +476,10 @@
     spot_ref[3:6, 0:P_OWN] = normal_ref[...].astype(jnp.float32)
     fresh_ref[...] = jnp.zeros_like(fresh_ref)
     load.wait()
+    for tile in range(field_ref.shape[2] // LANES):
+        for number in range(19):
+            lanes = slice(tile * LANES, (tile + 1) * LANES)
+            keep_rim(rim_ref, number, tile, field_ref[number, :, lanes])
 
     def swap(source_of, into_ref, send_sems, got_sems, distance):
         peer = lax.rem(me + distance, blocks)
@@ -512,7 +530,9 @@
 
     def one_step(step):
         got_ref = got_odd if step % 2 else got_even
-        collide_all(field_ref, rolled_ref, moving_ref, edge_ref, draft_ref)
+        collide_rim(rim_ref, edge_ref)
+        if step == 0:
+            collide_all(field_ref, rolled_ref, moving_ref, draft_ref)
         if step == 0:
             pl.semaphore_wait(barrier, blocks + ring - 2)
         edges = [
@@ -528,6 +548,8 @@
         ]
         for copy in edges:
             copy.start()
+        if step > 0:
+            collide_all(field_ref, rolled_ref, moving_ref, draft_ref)
         for copy in edges:
             copy.wait()
         pack_moving(moving_ref, near_ref.at[step], draft_ref, piece_ref)
@@ -562,7 +584,9 @@
             every(lambda distance: past_copy(distance).wait())
             settle_history(past_got, flat_ref, choose_ref, table_ref, partial_ref)
         every(lambda distance: copy_to(distance).wait())
-        finish_step(face, edge, got_ref, rolled_ref, field_ref, density_ref.at[step])
+        finish_step(
+            face, edge, got_ref, rolled_ref, field_ref, rim_ref, density_ref.at[step], step == STEPS - 1
+        )
 
     for step in range(STEPS):
         one_step(step)
@@ -689,6 +713,7 @@
             pltpu.VMEM((STEPS, slab_depth, lane_count), wide),
             pltpu.VMEM((tiles + 2, 19, slab_depth, LANES), wide),
             pltpu.VMEM((tiles, len(x_order), slab_depth, LANES), wide),
+            pltpu.VMEM((19, 2 * tiles, LANES), wide),
             pltpu.VMEM((2, 5, tiles, LANES), wide),
             pltpu.VMEM((STEPS, 2, 5, tiles, LANES), wide),
             pltpu.VMEM((4, slab_depth, FACE), wide),

time: 63.7 us -> 62.2 us (0.976)
  Pallas kernels: 59.1 us -> 57.7 us
    pallas_call x1, Pallas kernels: 59.1 us -> 57.7 us  [body(): pl.pallas_call(functools.partial(window_kernel, blocks, ring), out_shape=...]
where the time goes in v5:
time: 62.2 us; the launch traced here: 62 us
  Pallas kernels  57.7 us (93%)
  local copies, waits for them, and re-layouts  3.08 us (5%)
  between operations  1.3 us (2%)
    pallas_call x1, Pallas kernels, body(): pl.pallas_call(functools.partial(window_kernel, blocks, ring), out_shape=...  57.7 us
    unnamed x4, local copies, waits for them, and re-layouts  3.08 us

profile of v5, /device:TPU:0, one launch (start us, length us, event | category | flops | bytes accessed | tf_op | source)
XLA Modules:
  0.0 62.0 jit_solution(5346531970363167440)
XLA Ops:
  1.3 57.7 %shard_map.131 = (f32[19,16,1024]{2,1,0:T(8,128)}, f32[32,128]{1,0:T(8,128)}) custom-call(s32[1,4]{1,0:T(1,128)} %face_ref.1, s32[1,4]{1,0:T(1,128)} %rim_face_ref.1, s32[1]{0:T(128)S(6)} %copy.16.count_ref, f32[19,16,1024]{2,1,0:T(8,128)} %bitcast.6, s32[1,128]{1,0:T(1,128)} %bitcast.8, s32[1,128]{1,0:T(1,128)} %bitcast.9, bf16[128,512]{1,0:T(8,128)(2,1)} %history_ref.1, ...), custom_call_target="tpu_custom_call" | custom-call | tf_op jit(solution)/shard_map/pallas_call | solution.py:703
  58.9 0.0 copy-start
  59.0 2.5 %copy.17 = f32[1,19,16,1024]{3,2,1,0:T(8,128)} copy(f32[1,19,16,1024]{3,2,1,0:T(8,128)} %bitcast.5) | data formatting | bytes 2490368
  61.4 0.0 copy-done
  61.4 0.6 copy.18
Async XLA Ops:
  58.9 2.5 %copy-start = (f32[32,128]{1,0:T(8,128)S(1)}, f32[32,128]{1,0:T(8,128)}, u32[]{:S(2)}) copy-start(f32[32,128]{1,0:T(8,128)} %get-tuple-element.5) | copy-start | bytes 49156

commit v6 on v5

--- a/solution.py
+++ b/solution.py
@@ -412,11 +412,12 @@
         for start in range(0, panels, 32):
             rows = slice(start, start + 32)
             old_cos, old_sin, now_cos, now_sin, twice, ratio = [wave_ref[i, rows] for i in range(6)]
+            nearer = ratio.astype(jnp.bfloat16)
             for number in range(span):
-                near = [now_cos, now_sin, ratio * now_cos, ratio * now_sin]
-                for part, value in enumerate(near):
+                pair = [now_cos.astype(jnp.bfloat16), now_sin.astype(jnp.bfloat16)]
+                for part, value in enumerate(pair + [nearer * value for value in pair]):
                     into = slice(part * panels + start, part * panels + start + 32)
-                    held_ref[number, into] = value.astype(jnp.bfloat16)
+                    held_ref[number, into] = value
                 if first + number + 1 < BINS:
                     old_cos, now_cos = now_cos, twice * now_cos - old_cos
                     old_sin, now_sin = now_sin, twice * now_sin - old_sin

time: 62.2 us -> 61.7 us (level)
  no operation moved by 1% of the time
where the time goes in v6:
time: 61.7 us; the launch traced here: 61.5 us
  Pallas kernels  57.1 us (93%)
  local copies, waits for them, and re-layouts  3.08 us (5%)
  between operations  1.3 us (2%)
    pallas_call x1, Pallas kernels, body(): pl.pallas_call(functools.partial(window_kernel, blocks, ring), out_shape=...  57.1 us
    unnamed x4, local copies, waits for them, and re-layouts  3.08 us

profile of v6, /device:TPU:0, one launch (start us, length us, event | category | flops | bytes accessed | tf_op | source)
XLA Modules:
  0.0 61.5 jit_solution(2324339615821086843)
XLA Ops:
  1.3 57.1 %shard_map.131 = (f32[19,16,1024]{2,1,0:T(8,128)}, f32[32,128]{1,0:T(8,128)}) custom-call(s32[1,4]{1,0:T(1,128)} %face_ref.1, s32[1,4]{1,0:T(1,128)} %rim_face_ref.1, s32[1]{0:T(128)S(6)} %copy.16.count_ref, f32[19,16,1024]{2,1,0:T(8,128)} %bitcast.6, s32[1,128]{1,0:T(1,128)} %bitcast.8, s32[1,128]{1,0:T(1,128)} %bitcast.9, bf16[128,512]{1,0:T(8,128)(2,1)} %history_ref.1, ...), custom_call_target="tpu_custom_call" | custom-call | tf_op jit(solution)/shard_map/pallas_call | solution.py:704
  58.4 0.0 copy-start
  58.4 2.5 %copy.17 = f32[1,19,16,1024]{3,2,1,0:T(8,128)} copy(f32[1,19,16,1024]{3,2,1,0:T(8,128)} %bitcast.5) | data formatting | bytes 2490368
  60.9 0.0 copy-done
  60.9 0.6 copy.18
Async XLA Ops:
  58.4 2.5 %copy-start = (f32[32,128]{1,0:T(8,128)S(1)}, f32[32,128]{1,0:T(8,128)}, u32[]{:S(2)}) copy-start(f32[32,128]{1,0:T(8,128)} %get-tuple-element.5) | copy-start | bytes 49156

commit v7 on v6

--- a/solution.py
+++ b/solution.py
@@ -738,10 +738,10 @@
             pltpu.VMEM((8, LANES), wide),
             pltpu.VMEM((ring, 8, LANES), wide),
             pltpu.VMEM((listeners // width, 6, ring * P_OWN, width), wide),
-            pltpu.VMEM((4 * ring * P_OWN // LANES, BINS * 8, LANES), wide),
+            pltpu.VMEM((4 * ring * P_OWN // LANES, BINS * 8 + 8, LANES), wide),
             pltpu.VMEM((8, 4 * ring * P_OWN, width), half),
             pltpu.VMEM((8, 4 * ring * P_OWN, width), half),
-            pltpu.VMEM((width // LANES, BINS * 8, LANES), wide),
+            pltpu.VMEM((width // LANES, BINS * 8 + 8, LANES), wide),
             pltpu.VMEM((width // LANES, 2 * BINS, LANES), wide),
             pltpu.VMEM((blocks, chunk, 2 * BINS), wide),
             pltpu.VMEM((blocks, chunk, 2 * BINS), wide),

time: 61.7 us -> 61.7 us (level)
  no operation moved by 1% of the time
where the time goes in v7:
time: 61.7 us; the launch traced here: 61.5 us
  Pallas kernels  57.1 us (93%)
  local copies, waits for them, and re-layouts  3.08 us (5%)
  between operations  1.3 us (2%)
    pallas_call x1, Pallas kernels, body(): pl.pallas_call(functools.partial(window_kernel, blocks, ring), out_shape=...  57.1 us
    unnamed x4, local copies, waits for them, and re-layouts  3.08 us

profile of v7, /device:TPU:0, one launch (start us, length us, event | category | flops | bytes accessed | tf_op | source)
XLA Modules:
  0.0 61.5 jit_solution(7237968165254990435)
XLA Ops:
  1.3 57.1 %shard_map.131 = (f32[19,16,1024]{2,1,0:T(8,128)}, f32[32,128]{1,0:T(8,128)}) custom-call(s32[1,4]{1,0:T(1,128)} %face_ref.1, s32[1,4]{1,0:T(1,128)} %rim_face_ref.1, s32[1]{0:T(128)S(6)} %copy.16.count_ref, f32[19,16,1024]{2,1,0:T(8,128)} %bitcast.6, s32[1,128]{1,0:T(1,128)} %bitcast.8, s32[1,128]{1,0:T(1,128)} %bitcast.9, bf16[128,512]{1,0:T(8,128)(2,1)} %history_ref.1, ...), custom_call_target="tpu_custom_call" | custom-call | tf_op jit(solution)/shard_map/pallas_call | solution.py:704
  58.4 0.0 copy-start
  58.4 2.5 %copy.17 = f32[1,19,16,1024]{3,2,1,0:T(8,128)} copy(f32[1,19,16,1024]{3,2,1,0:T(8,128)} %bitcast.5) | data formatting | bytes 2490368
  60.9 0.0 copy-done
  60.9 0.6 copy.18
Async XLA Ops:
  58.4 2.5 %copy-start = (f32[32,128]{1,0:T(8,128)S(1)}, f32[32,128]{1,0:T(8,128)}, u32[]{:S(2)}) copy-start(f32[32,128]{1,0:T(8,128)} %get-tuple-element.5) | copy-start | bytes 49156
